TPU v7x, 256 devices: a whole 4x4x8 slice. The times are simulated.
256 devices in a mesh: batch: 64 (over z, x, y_hi), chan: 4 (over y_lo, core).
Axes of the slice: x: 4, y: 4 (y_hi: 2, y_lo: 2; y = y_hi * 2 + y_lo), z: 8, core: 2. Of those that a mesh axis runs over, the one named last changes fastest.
Arguments:
- signal: float32 [1024, 32768], P('chan', 'batch'), may hold values from -6 to 6
- cotangent: float32 [1024, 32768], P('chan', 'batch'), may hold values from -6 to 6
- first_layer: float32 [33, 64], replicated, may hold values from -5 to 5
- second_layer: float32 [64, 1024], P(None, 'chan'), may hold values from -0.75 to 0.75
- decay_rate: float32 [1024], P('chan'), may hold values from 0.3 to 600
- skip_gain: float32 [1024], P('chan'), may hold values from -4 to 4
Outputs:
- input_grad: float32 [1024, 32768], P('chan', 'batch')
- first_grad: float32 [33, 64], replicated
- second_grad: float32 [64, 1024], P(None, 'chan')
- decay_grad: float32 [1024], P('chan')
- skip_grad: float32 [1024], P('chan')
All inputs are finite; a program needn't handle non-finite values.
Results may differ from a plain program's by a relative error of at most 0.0003.
Values sent between devices are 32-bit elements; how exact they have to be, the bound alone decides.
A program may use at most 128 MiB of HBM per device.

v0:
```python
import math

import jax
import jax.numpy as jnp
from jax import lax
from jax.sharding import PartitionSpec as P

ROWS = 256


precise = lax.Precision.HIGHEST
epsilon = 1e-06


def rows_first(arrays, axis, dims):
    turned = [jnp.moveaxis(a, dim, 0) for a, dim in zip(arrays, dims)]
    widths = [t[0].size for t in turned]
    both = jnp.concatenate([t.reshape(-1, w) for t, w in zip(turned, widths)], axis=1)
    result = lax.all_gather(both, axis, axis=0, tiled=True)
    parts = jnp.split(result, [sum(widths[:k]) for k in range(1, len(widths))], axis=1)
    return tuple(
        (
            jnp.moveaxis(b.reshape(-1, *t.shape[1:]), 0, dim)
            for b, t, dim in zip(parts, turned, dims)
        )
    )


def total_of_pieces(x, axis):
    return lax.all_gather(x, axis).sum(0)


def features(positions, length, band_count):
    band_index = jnp.arange(1, band_count + 1, dtype=jnp.int32)
    phase = (band_index[:, None] * positions[None, :] % length).astype(jnp.float32) * (
        2.0 * math.pi / length
    )
    linear = positions.astype(jnp.float32)[None, :] / length
    return jnp.concatenate([linear, jnp.cos(phase), jnp.sin(phase)], axis=0)


def make_filter(first_layer, columns, rates, positions, length):
    embed = features(positions, length, first_layer.shape[0] // 2)
    before = jnp.dot(first_layer.T, embed, precision=precise)
    basis = jnp.sin(before)
    fraction = positions.astype(jnp.float32) / length
    window = jnp.exp(-rates[:, None] * fraction[None, :])
    shaped = window * jnp.dot(columns.T, basis, precision=precise)
    return (embed, before, basis, fraction, window, shaped)


def dft_tables(rows):
    counter = jnp.arange(rows, dtype=jnp.int32)
    product = counter[:, None] * counter[None, :]
    angle = (product % rows).astype(jnp.float32) * (2.0 * math.pi / rows)
    twist = product.astype(jnp.float32) * (2.0 * math.pi / (rows * rows))
    return (jnp.cos(angle), jnp.sin(angle), jnp.cos(twist), jnp.sin(twist))


def right_product(values, matrix):
    return jnp.dot(values, matrix, precision=precise)


def forward(signal, tables):
    cos_rows, sin_rows, cos_twist, sin_twist = tables
    rows = cos_rows.shape[0]
    half = rows // 2
    blocks = signal.reshape(signal.shape[0], half, rows)
    first_re = jnp.einsum("cam,ak->ckm", blocks, cos_rows[:half], precision=precise)
    first_im = -jnp.einsum("cam,ak->ckm", blocks, sin_rows[:half], precision=precise)
    twist_re = first_re * cos_twist + first_im * sin_twist
    twist_im = first_im * cos_twist - first_re * sin_twist
    spec_re = right_product(twist_re, cos_rows) + right_product(twist_im, sin_rows)
    spec_im = right_product(twist_im, cos_rows) - right_product(twist_re, sin_rows)
    return (spec_re, spec_im)


def inverse(spec_re, spec_im, tables):
    cos_rows, sin_rows, cos_twist, sin_twist = tables
    rows = cos_rows.shape[0]
    half = rows // 2
    back_re = right_product(spec_re, cos_rows) - right_product(spec_im, sin_rows)
    back_im = right_product(spec_im, cos_rows) + right_product(spec_re, sin_rows)
    turn_re = back_re * cos_twist - back_im * sin_twist
    turn_im = back_im * cos_twist + back_re * sin_twist
    blocks = jnp.einsum("ak,ckm->cam", cos_rows[:half], turn_re, precision=precise) - jnp.einsum(
        "ak,ckm->cam", sin_rows[:half], turn_im, precision=precise
    )
    return blocks.reshape(blocks.shape[0], half * rows) / float(rows * rows)


def correlate(values, cotan, filt, tables):
    count = values.shape[0]
    every_re, every_im = forward(jnp.concatenate([values, cotan, filt], axis=0), tables)
    val_re, cot_re, filt_re = (every_re[:count], every_re[count : 2 * count], every_re[2 * count :])
    val_im, cot_im, filt_im = (every_im[:count], every_im[count : 2 * count], every_im[2 * count :])
    prod_re = jnp.concatenate(
        [filt_re * cot_re + filt_im * cot_im, val_re * cot_re + val_im * cot_im], axis=0
    )
    prod_im = jnp.concatenate(
        [filt_re * cot_im - filt_im * cot_re, val_re * cot_im - val_im * cot_re], axis=0
    )
    both = inverse(prod_re, prod_im, tables)
    return (both[:count], both[count:])


def local(signal, cotangent, first_layer, second_layer, decay_rate, skip_gain):
    groups = lax.axis_size("batch")
    place = lax.axis_index("batch")
    width_dev = signal.shape[0]
    local_len = signal.shape[1]
    length = local_len * groups
    factor = 1.0 / math.sqrt(length)
    tables = dft_tables(ROWS)
    narrow = width_dev // groups
    spread_val, spread_cot = (
        lax.all_to_all(signal, "batch", split_axis=0, concat_axis=1, tiled=True),
        lax.all_to_all(cotangent, "batch", split_axis=0, concat_axis=1, tiled=True),
    )
    positions = jnp.arange(length, dtype=jnp.int32)
    columns = lax.dynamic_slice_in_dim(second_layer, place * narrow, narrow, 1)
    rates = lax.dynamic_slice_in_dim(decay_rate, place * narrow, narrow, 0)
    gains = lax.dynamic_slice_in_dim(skip_gain, place * narrow, narrow, 0)
    embed, before, basis, fraction, window, shaped = make_filter(
        first_layer, columns, rates, positions, length
    )
    norms = jnp.sqrt(jnp.sum(shaped * shaped, axis=1, keepdims=True) + epsilon)
    filt = shaped / norms
    in_grad, filt_grad = correlate(spread_val, spread_cot, filt, tables)
    in_grad = in_grad + gains[:, None] * spread_cot
    dfilt = factor * filt_grad
    skip_part = factor * jnp.sum(spread_cot * spread_val, axis=1)
    project = jnp.sum(filt * dfilt, axis=1, keepdims=True)
    draw = (dfilt - filt * project) / norms
    decay_part = -jnp.sum(draw * shaped * fraction[None, :], axis=1)
    dmix = draw * window
    second_part = jnp.dot(basis, dmix.T, precision=precise)
    dbasis = jnp.dot(columns, dmix, precision=precise)
    input_grad = lax.all_to_all(in_grad, "batch", split_axis=1, concat_axis=0, tiled=True)
    second_grad, decay_grad, skip_grad = rows_first(
        (second_part, decay_part, skip_part), "batch", (1, 0, 0)
    )
    first_part = jnp.dot(embed, (jnp.cos(before) * dbasis).T, precision=precise)
    first_grad = total_of_pieces(first_part, ("batch", "chan"))
    return (input_grad, first_grad, second_grad, decay_grad, skip_grad)


def solution(mesh):
    placed = (P("chan", "batch"), P("chan", "batch"), P(), P(None, "chan"), P("chan"), P("chan"))
    return jax.shard_map(
        local,
        mesh=mesh,
        in_specs=placed,
        out_specs=(P("chan", "batch"), P(), P(None, "chan"), P("chan"), P("chan")),
        check_vma=False,
    )
```

profile of v0, /device:TPU:8, one launch (start us, length us, event | category | flops | bytes accessed | tf_op | source)
XLA Modules:
  0.0 422.9 jit_solution(8014057047468033321)
XLA Ops:
  9.2 13.8 %all-to-all-start = ((f32[64,4,512]{2,1,0:T(4,128)}), f32[64,4,512]{2,1,0:T(4,128)S(1)}, u32[]{:S(2)}, u32[]{:S(2)}) async-start(f32[64,4,512]{2,1,0:T(4,128)} %all_to_all.40), calls=%async_computation | async-start | bytes 1048576 | tf_op jit(solution)/shard_map/all_to_all | solution.py:117
  25.2 9.6 %fusion.51 = (f32[16,32768]{1,0:T(8,128)S(1)}, f32[16,32768]{1,0:T(8,128)}) fusion(s32[16]{0:T(128)S(1)} %iota_add_fusion), kind=kLoop, calls=%fused_computation.55 | loop fusion | flops 7340032 | bytes 4194368 | tf_op jit(solution)/shard_map/cos | solution.py:39
  34.9 38.5 %fusion.131 = (f32[32768,64]{0,1:T(8,128)S(1)}, f32[32768,64]{0,1:T(8,128)}) fusion(f32[33,64]{1,0:T(8,128)S(1)} %copy-done.8, f32[16,32768]{1,0:T(8,128)} %get-tuple-element.16, f32[16,32768]{1,0:T(8,128)S(1)} %get-tuple-element.15, f32[1,32768]{1,0:T(1,128)S(1)} %convert_multiply_fusion.1), kind=kOutput, calls=%fused_computation.152 | convolution fusion | flops 832634880 | bytes 21111040 | tf_op jit(solution)/shard_map/dot_general | solution.py:44
  73.4 4.2 multiply_reduce_fusion.3
  77.7 13.0 %all-to-all-start.1 = ((f32[64,4,512]{2,1,0:T(4,128)}), f32[64,4,512]{2,1,0:T(4,128)}, u32[]{:S(2)}, u32[]{:S(2)}) async-start(f32[64,4,512]{2,1,0:T(4,128)} %all_to_all.43), calls=%async_computation.1 | async-start | bytes 1048576 | tf_op jit(solution)/shard_map/all_to_all | solution.py:118
  104.6 4.9 %all-to-all-done.1 = f32[64,4,512]{2,1,0:T(4,128)} async-done(((f32[64,4,512]{2,1,0:T(4,128)}), f32[64,4,512]{2,1,0:T(4,128)}, u32[]{:S(2)}, u32[]{:S(2)}) %all-to-all-start.1) | async-done | bytes 524320 | tf_op jit(solution)/shard_map/all_to_all | solution.py:118
  116.8 2.6 fusion.87
  119.5 2.6 fusion.86
  122.1 4.0 fusion.2
  126.2 3.8 fusion.4
  130.0 3.8 fusion.27
  133.8 4.2 fusion.24
  138.6 2.9 fusion.30
  141.5 2.8 fusion.31
  144.3 2.9 fusion.35
  147.2 3.0 fusion.34
  150.3 3.6 fusion.13
  153.9 3.6 fusion.42
  161.1 36.7 %convolution_multiply_fusion = f32[64,32768]{1,0:T(8,128)S(1)} fusion(f32[32768,64]{0,1:T(8,128)} %get-tuple-element.18, f32[4,32768]{1,0:T(4,128)S(1)} %get-tuple-element.6, f32[32768]{0:T(1024)S(1)} %convert_multiply_fusion.2, f32[4]{0:T(128)S(1)} %dynamic-slice_negate_fusion, f32[64,256]{1,0:T(8,128)S(1)} %copy-done, s32[]{:T(128)S(6)} %select_n.43), kind=kOutput, calls=%fused_computation | convolution fusion | flops 103022592 | bytes 17465860 | tf_op jit(solution)/shard_map/dot_general | solution.py:138
  197.8 7.4 %fusion.45 = f32[1,33,64]{2,1,0:T(8,128)} fusion(f32[64,32768]{1,0:T(8,128)S(1)} %convolution_multiply_fusion, f32[16,32768]{1,0:T(8,128)S(1)} %copy-done.2, f32[16,32768]{1,0:T(8,128)S(1)} %get-tuple-element.15, f32[1,32768]{1,0:T(1,128)S(1)} %convert_multiply_fusion.1), kind=kOutput, calls=%fused_computation.45 | convolution fusion | flops 832634880 | bytes 12722432 | tf_op jit(solution)/shard_map/dot_general | solution.py:143
  209.4 8.0 %all-to-all-start.2 = ((f32[4,64,512]{2,0,1:T(4,128)}), f32[4,64,512]{2,0,1:T(4,128)S(1)}, u32[]{:S(2)}, u32[]{:S(2)}) async-start(f32[4,64,512]{2,0,1:T(4,128)} %bitcast.18), calls=%async_computation.2 | async-start | bytes 1048576 | tf_op jit(solution)/shard_map/all_to_all | solution.py:139
  217.5 9.0 %fusion.53 = f32[4,64]{1,0:T(4,128)S(1)} fusion(f32[32768,64]{0,1:T(8,128)} %copy-done.1, f32[4,32768]{1,0:T(4,128)S(1)} %get-tuple-element.6, f32[32768]{0:T(1024)S(1)} %convert_multiply_fusion.2, f32[4]{0:T(128)S(1)} %dynamic-slice_negate_fusion), kind=kOutput, calls=%fused_computation.69 | convolution fusion | flops 100925440 | bytes 9045008 | tf_op jit(solution)/shard_map/dot_general | solution.py:137
  226.6 182.5 %all-gather.2 = f32[64,4,66]{2,1,0:T(4,128)S(1)} all-gather(f32[1,4,66]{2,1,0:T(4,128)S(1)} %maximum_bitcast_fusion), channel_id=1, replica_groups=mesh['batch'=64,'chan'=4] {'batch'}, dimensions={0}, use_global_device_ids=true | all-gather | bytes 68640 | tf_op jit(solution)/shard_map/all_gather | solution.py:19
  412.2 3.6 reduce_sum.47
  (69 shorter events, 37.1 us)
Async XLA Ops:
  7.2 66.2 %copy-start = (f32[64,256]{1,0:T(8,128)S(1)}, f32[64,256]{1,0:T(8,128)}, u32[]{:S(2)}) copy-start(f32[64,256]{1,0:T(8,128)} %param.9) | copy-start | bytes 196612
  9.2 25.6 %copy-start.9 = (f32[256]{0:T(256)S(1)}, f32[256]{0:T(256)}, u32[]{:S(2)}) copy-start(f32[256]{0:T(256)} %param.10) | copy-start | bytes 3076
  9.2 25.7 %copy-start.8 = (f32[33,64]{1,0:T(8,128)S(1)}, f32[33,64]{1,0:T(8,128)}, u32[]{:S(2)}) copy-start(f32[33,64]{1,0:T(8,128)} %param.8) | copy-start | bytes 25348
  9.2 68.5 %all-to-all-start = ((f32[64,4,512]{2,1,0:T(4,128)}), f32[64,4,512]{2,1,0:T(4,128)S(1)}, u32[]{:S(2)}, u32[]{:S(2)}) async-start(f32[64,4,512]{2,1,0:T(4,128)} %all_to_all.40), calls=%async_computation | async-start | bytes 1048576 | tf_op jit(solution)/shard_map/all_to_all | solution.py:117
  73.4 4.3 %copy-start.1 = (f32[32768,64]{0,1:T(8,128)}, f32[32768,64]{0,1:T(8,128)S(1)}, u32[]{:S(2)}) copy-start(f32[32768,64]{0,1:T(8,128)S(1)} %get-tuple-element.17) | copy-start | bytes 25165828
  73.4 18.5 %copy-start.10 = (f32[256]{0:T(256)S(1)}, f32[256]{0:T(256)}, u32[]{:S(2)}) copy-start(f32[256]{0:T(256)} %param.11) | copy-start | bytes 3076
  77.7 14.3 %copy-start.3 = (f32[64,4,512]{2,1,0:T(4,128)}, f32[64,4,512]{2,1,0:T(4,128)S(1)}, u32[]{:S(2)}) copy-start(f32[64,4,512]{2,1,0:T(4,128)S(1)} %all-to-all-done) | copy-start | bytes 1572868
  77.7 31.8 %all-to-all-start.1 = ((f32[64,4,512]{2,1,0:T(4,128)}), f32[64,4,512]{2,1,0:T(4,128)}, u32[]{:S(2)}, u32[]{:S(2)}) async-start(f32[64,4,512]{2,1,0:T(4,128)} %all_to_all.43), calls=%async_computation.1 | async-start | bytes 1048576 | tf_op jit(solution)/shard_map/all_to_all | solution.py:118
  90.7 321.5 %all-gather.5.cloned.1.call-start = ((), (), s32[]{:S(2)}) async-start(), calls=%async_computation.3 | async-start | bytes 5263360 | tf_op jit(solution)/shard_map/all_gather | solution.py:30
  113.4 3.4 copy-start.7
  115.6 3.8 copy-start.6
  161.1 36.7 %copy-start.2 = (f32[16,32768]{1,0:T(8,128)S(1)}, f32[16,32768]{1,0:T(8,128)}, u32[]{:S(2)}) copy-start(f32[16,32768]{1,0:T(8,128)} %get-tuple-element.16) | copy-start | bytes 6291460
  197.8 7.4 %copy-start.5 = (f32[4,128,256]{1,2,0:T(8,128)S(1)}, f32[4,128,256]{1,2,0:T(8,128)}, u32[]{:S(2)}) copy-start(f32[4,128,256]{1,2,0:T(8,128)} %get-tuple-element.12) | copy-start | bytes 1572868
  205.2 2.6 copy-start.4
  209.4 201.8 %all-to-all-start.2 = ((f32[4,64,512]{2,0,1:T(4,128)}), f32[4,64,512]{2,0,1:T(4,128)S(1)}, u32[]{:S(2)}, u32[]{:S(2)}) async-start(f32[4,64,512]{2,0,1:T(4,128)} %bitcast.18), calls=%async_computation.2 | async-start | bytes 1048576 | tf_op jit(solution)/shard_map/all_to_all | solution.py:139
Sparse Core Ops, SparseCore 0:
  205.3 113.1 all-gather.4
where the time goes:
time: 431 us; the launch traced here: 423 us
  blocking collectives  183 us (42%)
  matrix products  136 us (32%)
  starting transfers between devices  35 us (8%)
  other arithmetic  27.1 us (6%)
  local copies, waits for them, and re-layouts  22.9 us (5%)
  between operations  14.6 us (3%)
  waiting for transfers between devices  4.92 us (1%)
    all_gather x1, blocking collectives, rows_first(): result = lax.all_gather(both, axis, axis=0, tiled=True)  183 us
    dot_general x1, matrix products, make_filter(): before = jnp.dot(first_layer.T, embed, precision=precise)  38.5 us
    dot_general x1, matrix products, local(): dbasis = jnp.dot(columns, dmix, precision=precise)  36.7 us
    dot_general x8, matrix products, right_product(): return jnp.dot(values, matrix, precision=precise)  27.5 us
    all_to_all x1, starting transfers between devices, local(): lax.all_to_all(signal, 'batch', split_axis=0, concat_axis=1, tiled=True)  13.8 us
    all_to_all x1, starting transfers between devices, local(): lax.all_to_all(cotangent, 'batch', split_axis=0, concat_axis=1, tiled=True)  13 us
    cos x1, other arithmetic, features(): return jnp.concatenate([linear, jnp.cos(phase), jnp.sin(phase)], axis=0)  9.62 us
    dot_general x1, matrix products, local(): second_part = jnp.dot(basis, dmix.T, precision=precise)  9.01 us
  transfers between devices with their start and end apart: 4, of which 1 were waited for; matrix products, arithmetic and copies ran while one was open for 19% of the time, Pallas kernels for 0%

commit v1 on v0

v1 whole, which is shorter than its diff:
```python
import functools
import math

import jax
import jax.numpy as jnp
import numpy as np
from jax import lax
from jax.experimental import pallas as pl
from jax.experimental.pallas import tpu as pltpu
from jax.sharding import PartitionSpec as P

GROUPS = 64
PEERS = 4
NARROW = 4
LENGTH = 32768
LOCAL = LENGTH // GROUPS
ORDER = 64
BANDS = 16
EMBED = 33
A = 128
M = 256
TERMS = 2 * BANDS + 2
FACTOR = 1.0 / math.sqrt(LENGTH)
EPSILON = 1e-06
F32 = jnp.float32
BF16 = jnp.bfloat16
MESH = pl.DeviceIdType.MESH
KK = 4


def split_np(x):
    hi = np.asarray(x, np.float32).astype(jnp.bfloat16)
    lo = (np.asarray(x, np.float64) - hi.astype(np.float64)).astype(jnp.bfloat16)
    return hi, lo


@functools.cache
def tables():
    row = np.arange(A)
    place = 2 * (row % 64) + row // 64
    k1 = np.arange(A)[:, None] + 0.25
    m = np.arange(M)
    phase = 2 * np.pi * k1 * place[None, :] / A
    first = np.concatenate([np.cos(phase), -np.sin(phase)], axis=0)
    twist = -2 * np.pi * k1 * m[None, :] / LENGTH
    grid = 2 * np.pi * (np.outer(m, m) % M) / M
    c, s = np.cos(grid), np.sin(grid)
    second = np.block([[c, -s], [s, c]])
    last = np.concatenate([np.cos(phase), -np.sin(phase)], axis=0).T / LENGTH
    out = {}
    out["t1h"], out["t1l"] = split_np(first)
    out["dh"], out["dl"] = split_np(second)
    out["eh"], out["el"] = split_np(second.T)
    out["t2h"], out["t2l"] = split_np(last)
    out["twr"] = np.cos(twist).astype(np.float32)
    out["twi"] = np.sin(twist).astype(np.float32)
    b = np.arange(1, BANDS + 1)
    alpha = 2 * np.pi * np.outer(place, b) / A
    beta = 2 * np.pi * np.outer(b, m) / LENGTH
    ones = np.ones((A, 1))
    ca = np.concatenate([np.cos(alpha), np.cos(alpha), place[:, None] / A, ones], axis=1)
    sa = np.concatenate([np.sin(alpha), np.sin(alpha), 0 * ones, 0 * ones], axis=1)
    q = np.concatenate([np.cos(beta), np.sin(beta), np.ones((1, M)), m[None, :] / LENGTH], axis=0)
    wide = lambda x: np.pad(np.tile(x, (1, 6)), ((0, 0), (0, 256 - 6 * TERMS))).astype(np.float32)
    out["ca"], out["sa"] = wide(ca), wide(sa)
    qh, rest = split_np(q)[0], None
    qm = (q - qh.astype(np.float64)).astype(jnp.bfloat16)
    ql = (q - qh.astype(np.float64) - qm.astype(np.float64)).astype(jnp.bfloat16)
    q6 = np.concatenate([qh, qm, ql, qh, qm, qh], axis=0)
    out["q6"] = np.pad(q6, ((0, 256 - 6 * TERMS), (0, 0)))
    qb = np.zeros((2 * M, 128), jnp.bfloat16)
    qb[:M, :TERMS] = qh.T
    qb[:M, TERMS : 2 * TERMS] = qm.T
    qb[M:, :TERMS] = qh.T
    out["qb"] = qb
    e1 = np.zeros((128, 64), np.float32)
    e2 = np.zeros((128, 64), np.float32)
    for copy in range(2):
        o = copy * TERMS
        for i in range(BANDS):
            e1[o + i, 1 + i] = 1
            e1[o + BANDS + i, 1 + BANDS + i] = 1
            e2[o + i, 1 + BANDS + i] = 1
            e2[o + BANDS + i, 1 + i] = -1
        e1[o + 2 * BANDS, 0] = 1
        e1[o + 2 * BANDS + 1, 0] = 1
    zero = np.zeros_like(e1)
    out["ea"] = np.concatenate([np.concatenate([e1, zero], 1), np.concatenate([zero, e1], 1)], 0)
    out["eb"] = np.concatenate([np.concatenate([e2, zero], 1), np.concatenate([zero, e2], 1)], 0)
    return out


NAMES = ("t1h", "t1l", "dh", "dl", "eh", "el", "t2h", "t2l", "twr", "twi", "ca", "sa", "q6", "qb", "ea", "eb")


def halves(x):
    hi = x.astype(BF16)
    return hi, (x - hi.astype(F32)).astype(BF16)


def dot(a, b):
    return jnp.dot(a, b, preferred_element_type=F32)


def mm3(ah, al, bh, bl):
    return dot(ah, bh) + dot(al, bh) + dot(ah, bl)


def sin_cos(x):
    magic = 12582912.0
    turns = (x * (0.5 / math.pi) + magic) - magic
    h = x * 0.5 - turns * 3.140625
    h = h - turns * 9.67502593994140625e-4
    h = h - turns * 1.509957990978376e-07
    z = h * h
    s = 2.59701174e-06
    s = s * z - 1.98052345e-04
    s = s * z + 8.33299813e-03
    s = s * z - 1.66666563e-01
    s = h + h * (z * s)
    c = -2.61670784e-07
    c = c * z + 2.47680152e-05
    c = c * z - 1.38885497e-03
    c = c * z + 4.16666549e-02
    c = c * z - 0.5
    c = c * z + 1.0
    twice = s + s
    return twice * c, 1.0 - twice * s


def kernel(comm, *refs):
    it = iter(refs)
    sig, cot, u_ref, v_ref, cols, scal = (next(it) for _ in range(6))
    t = {name: next(it) for name in NAMES}
    out, gath_out, first_out = (next(it) for _ in range(3))
    (s_send, c_send, s_recv, c_recv, y_send, y_recv) = (next(it) for _ in range(6))
    (basis, cosb, pbuf, bbuf, raw, dmix) = (next(it) for _ in range(6))
    (xh, xl, gh, gl, spec_f, spec_c, spec_s, wbuf) = (next(it) for _ in range(8))
    (mid, gath, sgs, ug, vg, red_a, red_b, red_c) = (next(it) for _ in range(8))
    (send_sem, recv_sem) = (next(it) for _ in range(2))

    if comm:
        bi = lax.axis_index("batch")
        ci = lax.axis_index("chan")
        barrier = pltpu.get_barrier_semaphore()

        def greet(i, _):
            pl.semaphore_signal(barrier, inc=1, device_id={"batch": lax.rem(bi + i, GROUPS)}, device_id_type=MESH)
            return 0

        lax.fori_loop(1, GROUPS, greet, 0)
        for i in range(1, PEERS):
            pl.semaphore_signal(barrier, inc=1, device_id={"chan": lax.rem(ci + i, PEERS)}, device_id_type=MESH)

    def spread(src, dst, slot, rows):
        mine = pl.ds(pl.multiple_of(bi * rows, rows), rows)

        def push(i, _):
            p = lax.rem(bi + i, GROUPS)
            pltpu.make_async_remote_copy(
                src_ref=src.at[pl.ds(pl.multiple_of(p * rows, rows), rows)],
                dst_ref=dst.at[mine],
                send_sem=send_sem.at[slot],
                recv_sem=recv_sem.at[slot],
                device_id={"batch": p},
                device_id_type=MESH,
            ).start()
            return 0

        lax.fori_loop(1, GROUPS, push, 0)
        dst[mine, :] = src[mine, :]

    def landed(dst, sem, slot, rows):
        part = dst.at[pl.ds(0, (GROUPS - 1) * rows)]
        pltpu.make_async_copy(part, part, sem.at[slot]).wait()

    if comm:
        for q in range(4):
            lanes = slice(q * 128, q * 128 + 128)
            c_send[pl.ds(q, 256, stride=4), :] = cot[:, lanes]
            s_send[pl.ds(q, 256, stride=4), :] = sig[:, lanes]
        pl.semaphore_wait(barrier, GROUPS - 1 + PEERS - 1)
        spread(c_send, c_recv, 0, 16)
        spread(s_send, s_recv, 1, 16)
    else:
        c_recv[...] = cot[...]
        s_recv[...] = sig[...]

    lane = lax.broadcasted_iota(jnp.int32, (1, 256), 1)
    raw[...] = jnp.zeros_like(raw)

    def hidden(step, _):
        for i in range(KK):
            k = step * KK + i
            for r in range(0, A, 32):
                rows = slice(r, r + 32)
                p = u_ref[pl.ds(k, 1), :] * t["ca"][rows, :] + v_ref[pl.ds(k, 1), :] * t["sa"][rows, :]
                hi = p.astype(BF16).astype(F32)
                rest = p - hi
                med = rest.astype(BF16).astype(F32)
                low = rest - med
                p = jnp.where(lane < 3 * TERMS, hi, jnp.where(lane < 5 * TERMS, med, low))
                pbuf[i * A + r : i * A + r + 32, :] = p.astype(BF16)
        bbuf[...] = dot(pbuf[...], t["q6"][...])

        for r in range(0, A, 16):
            rows = slice(r, r + 16)
            acc = [raw[c, rows, :] for c in range(NARROW)]
            for i in range(KK):
                k = step * KK + i
                sine, cosine = sin_cos(bbuf[i * A + r : i * A + r + 16, :])
                basis[k, rows, :] = sine
                cosb[k, rows, :] = cosine
                for c in range(NARROW):
                    acc[c] = acc[c] + sine * cols[k, c]
            for c in range(NARROW):
                raw[c, rows, :] = acc[c]
        return 0

    lax.fori_loop(0, ORDER // KK, hidden, 0)

    row = lax.broadcasted_iota(jnp.int32, (A, M), 0)
    col = lax.broadcasted_iota(jnp.int32, (A, M), 1)
    place = 512 * lax.rem(row, 64) + 256 * (row // 64) + col
    fraction = place.astype(F32) * (1.0 / LENGTH)

    def total(x):
        return jnp.sum(jnp.sum(x, axis=1, keepdims=True), axis=0, keepdims=True)

    def forward(load, spec):
        for c in range(NARROW):
            xh[...], xl[...] = halves(load(c))
            f = mm3(t["t1h"][...], t["t1l"][...], xh[...], xl[...])
            re, im = f[:A], f[A:]
            rows = slice(c * A, c * A + A)
            gh[rows, :M], gl[rows, :M] = halves(re * t["twr"][...] - im * t["twi"][...])
            gh[rows, M:], gl[rows, M:] = halves(re * t["twi"][...] + im * t["twr"][...])
        spec[...] = mm3(gh[...], gl[...], t["dh"][...], t["dl"][...])

    def inverse(one, two, store):
        for c in range(NARROW):
            rows = slice(c * A, c * A + A)
            r1, i1, r2, i2 = one[rows, :M], one[rows, M:], two[rows, :M], two[rows, M:]
            gh[rows, :M], gl[rows, :M] = halves(r1 * r2 + i1 * i2)
            gh[rows, M:], gl[rows, M:] = halves(r1 * i2 - i1 * r2)
        wbuf[...] = mm3(gh[...], gl[...], t["eh"][...], t["el"][...])
        for c in range(NARROW):
            rows = slice(c * A, c * A + A)
            re, im = wbuf[rows, :M], wbuf[rows, M:]
            mid[:A, :] = re * t["twr"][...] + im * t["twi"][...]
            mid[A:, :] = im * t["twr"][...] - re * t["twi"][...]
            h, low = halves(mid[...])
            store(c, mm3(t["t2h"][...], t["t2l"][...], h, low))

    def blocks_of(buf, c):
        parts = [
            [buf[pl.ds(4 * c + 2 * h + q, 64, stride=16), :] for q in range(2)] for h in range(2)
        ]
        return jnp.concatenate([jnp.concatenate(p, axis=1) for p in parts], axis=0)

    norms = []
    for c in range(NARROW):
        value = raw[c] * jnp.exp(-scal[0, c] * fraction)
        raw[c] = value
        norms.append(jnp.sqrt(total(value * value) + EPSILON))
    forward(lambda c: raw[c] / norms[c], spec_f)

    if comm:
        landed(c_recv, recv_sem, 0, 16)
    forward(lambda c: blocks_of(c_recv, c), spec_c)

    def store_grad(c, y):
        y = y + scal[1, c] * blocks_of(c_recv, c)
        for h in range(2):
            for q in range(2):
                y_send[pl.ds(4 * c + 2 * h + q, 64, stride=16), :] = y[h * 64 : h * 64 + 64, q * 128 : q * 128 + 128]

    inverse(spec_f, spec_c, store_grad)
    if comm:
        spread(y_send, y_recv, 2, 16)
        landed(s_recv, recv_sem, 1, 16)
    forward(lambda c: blocks_of(s_recv, c), spec_s)
    sgs[...] = jnp.zeros_like(sgs)

    def store_filter(c, y):
        dfilt = FACTOR * y
        norm = norms[c]
        value = raw[c]
        filt = value / norm
        project = total(filt * dfilt)
        draw = (dfilt - filt * project) / norm
        decay = -jnp.sum(draw * value * fraction, axis=0, keepdims=True)
        skip = FACTOR * jnp.sum(blocks_of(c_recv, c) * blocks_of(s_recv, c), axis=0, keepdims=True)
        sgs[c * 128 + 64 : c * 128 + 65, :] = decay[:, :128] + decay[:, 128:]
        sgs[c * 128 + 65 : c * 128 + 66, :] = skip[:, :128] + skip[:, 128:]
        dmix[c] = draw * jnp.exp(-scal[0, c] * fraction)

    inverse(spec_s, spec_c, store_filter)

    def hidden_back(step, _):
        sums = [[jnp.zeros((8, 128), F32) for _ in range(NARROW)] for _ in range(KK)]
        for r in range(0, A, 16):
            rows = slice(r, r + 16)
            d = [dmix[c, rows, :] for c in range(NARROW)]
            for i in range(KK):
                k = step * KK + i
                b = basis[k, rows, :]
                g = d[0] * cols[k, 0]
                for c in range(1, NARROW):
                    g = g + d[c] * cols[k, c]
                g = g * cosb[k, rows, :]
                ghi, glo = halves(g)
                gh[i * A + r : i * A + r + 16, :M] = ghi
                gh[i * A + r : i * A + r + 16, M:] = glo
                for c in range(NARROW):
                    e = b * d[c]
                    sums[i][c] = sums[i][c] + ((e[:8, :128] + e[:8, 128:]) + (e[8:, :128] + e[8:, 128:]))
        for i in range(KK):
            for c in range(NARROW):
                sgs[pl.ds(c * 128 + step * KK + i, 1), :] = jnp.sum(sums[i][c], axis=0, keepdims=True)
        hmat = dot(gh[...], t["qb"][...])
        for i in range(KK):
            part = hmat[i * A : i * A + A]
            ug[pl.ds(step * KK + i, 1), :] = jnp.sum(part * t["ca"][:, :128], axis=0, keepdims=True)
            vg[pl.ds(step * KK + i, 1), :] = jnp.sum(part * t["sa"][:, :128], axis=0, keepdims=True)
        return 0

    lax.fori_loop(0, ORDER // KK, hidden_back, 0)

    high = lax.Precision.HIGHEST
    hdot = lambda a, b: jnp.dot(a, b, precision=high, preferred_element_type=F32)
    first = (
        hdot(ug[:32, :], t["ea"][:128, :])
        + hdot(ug[32:, :], t["ea"][128:, :])
        + hdot(vg[:32, :], t["eb"][:128, :])
        + hdot(vg[32:, :], t["eb"][128:, :])
    )
    ones = jnp.ones((8, 128), F32)
    sums = [
        lax.dot_general(
            ones, sgs[c * 128 : c * 128 + 128, :], (((1,), (1,)), ((), ())), precision=high, preferred_element_type=F32
        )[:1]
        for c in range(NARROW)
    ]
    block = jnp.concatenate(sums, axis=0)

    if not comm:
        for q in range(4):
            out[:, q * 128 : q * 128 + 128] = y_send[pl.ds(q, 256, stride=4), :]
        gath_out[...] = jnp.zeros_like(gath_out)
        gath_out[0] = block
        first_out[...] = first
        return

    gath[pl.ds(bi, 1)] = block[None]

    def tell(i, _):
        pltpu.make_async_remote_copy(
            src_ref=gath.at[bi],
            dst_ref=gath.at[bi],
            send_sem=send_sem.at[3],
            recv_sem=recv_sem.at[3],
            device_id={"batch": lax.rem(bi + i, GROUPS)},
            device_id_type=MESH,
        ).start()
        return 0

    def stage(buf, slot, value, me, count, target):
        buf[pl.ds(me, 1)] = value[None]
        for i in range(1, count):
            pltpu.make_async_remote_copy(
                src_ref=buf.at[me],
                dst_ref=buf.at[me],
                send_sem=send_sem.at[slot],
                recv_sem=recv_sem.at[slot],
                device_id=target(lax.rem(me + i, count)),
                device_id_type=MESH,
            ).start()
        if slot == 4:
            lax.fori_loop(1, GROUPS, tell, 0)
        part = buf.at[pl.ds(0, count - 1)]
        pltpu.make_async_copy(part, part, recv_sem.at[slot]).wait()
        pltpu.make_async_copy(part, part, send_sem.at[slot]).wait()
        value = buf[0]
        for i in range(1, count):
            value = value + buf[i]
        return value

    zi, xy = bi // 8, lax.rem(bi, 8)
    first = stage(red_a, 4, first, ci, PEERS, lambda p: {"chan": p})
    first = stage(red_b, 5, first, zi, 8, lambda p: {"batch": p * 8 + xy})
    first = stage(red_c, 6, first, xy, 8, lambda p: {"batch": zi * 8 + p})
    first_out[...] = first

    landed(y_recv, recv_sem, 2, 16)
    for q in range(4):
        out[:, q * 128 : q * 128 + 128] = y_recv[pl.ds(q, 256, stride=4), :]
    landed(gath, recv_sem, 3, 1)
    gath_out[...] = gath[...]
    landed(c_send, send_sem, 0, 16)
    landed(s_send, send_sem, 1, 16)
    landed(y_send, send_sem, 2, 16)
    landed(gath, send_sem, 3, 1)


def call(comm, sig, cot, u, v, cols, scal):
    vmem = pl.BlockSpec(memory_space=pltpu.VMEM)
    smem = pl.BlockSpec(memory_space=pltpu.SMEM)
    t = tables()
    rows = GROUPS * 16
    line = lambda: pltpu.VMEM((rows, 128), F32)
    scratch = [line() for _ in range(6)]
    scratch += [
        pltpu.VMEM((ORDER, A, M), F32),
        pltpu.VMEM((ORDER, A, M), F32),
        pltpu.VMEM((KK * A, 256), BF16),
        pltpu.VMEM((KK * A, M), F32),
        pltpu.VMEM((NARROW, A, M), F32),
        pltpu.VMEM((NARROW, A, M), F32),
        pltpu.VMEM((A, M), BF16),
        pltpu.VMEM((A, M), BF16),
        pltpu.VMEM((NARROW * A, 2 * M), BF16),
        pltpu.VMEM((NARROW * A, 2 * M), BF16),
        pltpu.VMEM((NARROW * A, 2 * M), F32),
        pltpu.VMEM((NARROW * A, 2 * M), F32),
        pltpu.VMEM((NARROW * A, 2 * M), F32),
        pltpu.VMEM((NARROW * A, 2 * M), F32),
        pltpu.VMEM((2 * A, M), F32),
        pltpu.VMEM((GROUPS, NARROW, 128), F32),
        pltpu.VMEM((NARROW * 128, 128), F32),
        pltpu.VMEM((ORDER, 128), F32),
        pltpu.VMEM((ORDER, 128), F32),
        pltpu.VMEM((PEERS, 32, 128), F32),
        pltpu.VMEM((8, 32, 128), F32),
        pltpu.VMEM((8, 32, 128), F32),
        pltpu.SemaphoreType.DMA((7,)),
        pltpu.SemaphoreType.DMA((7,)),
    ]
    params = dict(vmem_limit_bytes=56 * 2**20)
    if comm:
        params.update(collective_id=0, has_side_effects=True)
    return pl.pallas_call(
        functools.partial(kernel, comm),
        out_shape=(
            jax.ShapeDtypeStruct((256, LOCAL), F32),
            jax.ShapeDtypeStruct((GROUPS, NARROW, 128), F32),
            jax.ShapeDtypeStruct((32, 128), F32),
        ),
        in_specs=[vmem] * 4 + [smem] * 2 + [vmem] * len(NAMES),
        out_specs=(vmem, vmem, vmem),
        scratch_shapes=scratch,
        compiler_params=pltpu.CompilerParams(**params),
        name="hyena_back",
    )(sig, cot, u, v, cols, scal, *[jnp.asarray(t[name]) for name in NAMES])


def terms(first_layer):
    linear = first_layer[:1]
    cosine, sine = first_layer[1 : 1 + BANDS], first_layer[1 + BANDS :]
    u = jnp.concatenate([cosine, sine, linear, linear], axis=0).T
    v = jnp.concatenate([sine, -cosine, 0 * linear, 0 * linear], axis=0).T
    wide = lambda x: jnp.pad(jnp.tile(x, (1, 6)), ((0, 0), (0, 256 - 6 * TERMS)))
    return wide(u), wide(v)


def local(signal, cotangent, first_layer, second_layer, decay_rate, skip_gain):
    start = lax.axis_index("batch") * NARROW
    u, v = terms(first_layer)
    cols = lax.dynamic_slice_in_dim(second_layer, start, NARROW, 1)
    scal = jnp.stack([lax.dynamic_slice_in_dim(x, start, NARROW, 0) for x in (decay_rate, skip_gain)])
    grad, gath, first = call(True, signal, cotangent, u, v, cols, scal)
    gath = gath.reshape(GROUPS * NARROW, 128)
    first_grad = jnp.concatenate([first[:, :EMBED], first[:, 64 : 64 + EMBED]], axis=0).T
    return grad, first_grad, gath[:, :ORDER].T, gath[:, ORDER], gath[:, ORDER + 1]


def solution(mesh):
    placed = (P("chan", "batch"), P("chan", "batch"), P(), P(None, "chan"), P("chan"), P("chan"))
    return jax.shard_map(
        local,
        mesh=mesh,
        in_specs=placed,
        out_specs=(P("chan", "batch"), P(), P(None, "chan"), P("chan"), P("chan")),
        check_vma=False,
    )
```

time: 431 us -> 81.6 us (0.19)
  the two profiles are of different devices: /device:TPU:8 before, /device:TPU:1 now
where the time goes in v1:
time: 81.6 us; the launch traced here: 81.4 us
  Pallas kernels  72.5 us (89%)
  local copies, waits for them, and re-layouts  7.47 us (9%)
    pallas_call x1, Pallas kernels, call(): pl.pallas_call(functools.partial(kernel, comm), out_shape=(jax.ShapeDtype...  72.5 us
    unnamed x17, local copies, waits for them, and re-layouts  4.25 us

profile of v1, /device:TPU:1, one launch (start us, length us, event | category | flops | bytes accessed | tf_op | source)
XLA Modules:
  0.0 81.4 jit_solution(10795782832892961446)
XLA Ops:
  0.6 0.0 copy-start
  0.7 0.0 copy-start.4
  0.7 0.0 copy-start.5
  0.7 0.7 copy-done.4
  1.4 0.0 copy-done.5
  1.4 0.1 dynamic-slice_bitcast_fusion
  1.5 0.6 pad_maximum_fusion.refs_5_
  2.0 0.0 copy-done
  2.0 0.7 constant_dynamic-slice_fusion.refs_4_
  2.7 0.0 copy-done.3
  2.8 0.1 copy.31
  2.9 0.6 pad.7.refs_2_
  3.6 0.1 copy.32
  3.7 0.6 pad.8.refs_3_
  4.3 72.5 %hyena_back.1 = (f32[256,512]{1,0:T(8,128)}, f32[64,4,128]{2,1,0:T(4,128)}, f32[32,128]{1,0:T(8,128)}) custom-call(f32[256,512]{1,0:T(8,128)} %refs_0_.1, f32[256,512]{1,0:T(8,128)} %refs_1_.1, f32[64,256]{1,0:T(8,128)} %pad.7.refs_2_, f32[64,256]{1,0:T(8,128)} %pad.8.refs_3_, f32[64,4]{1,0:T(8,128)} %constant_dynamic-slice_fusion.refs_4_, ...), custom_call_target="tpu_custom_call" | custom-call | tf_op jit(solution)/shard_map/hyena_back/pallas_call | solution.py:442
  76.8 0.0 copy-start.1
  76.8 0.9 %fusion.2 = (f32[32,33]{1,0:T(8,128)S(1)}, f32[32,33]{1,0:T(8,128)S(1)}) fusion(f32[32,128]{1,0:T(8,128)} %get-tuple-element.9), kind=kLoop, calls=%fused_computation.11 | loop fusion | bytes 16896 | tf_op jit(solution)/shard_map/slice | solution.py:473
  77.7 0.7 copy.36
  78.4 0.1 fusion
  78.6 0.6 copy.38
  79.2 0.6 copy.39
  79.8 0.7 copy.37
  80.6 0.0 copy-done.2
  80.6 0.8 copy.41
  (12 shorter events, 0.1 us)
Async XLA Ops:
  0.6 1.4 %copy-start = (f32[64,256]{1,0:T(8,128)S(1)}, f32[64,256]{1,0:T(8,128)}, u32[]{:S(2)}) copy-start(f32[64,256]{1,0:T(8,128)} %param.25) | copy-start | bytes 196612
  0.7 0.7 copy-start.4
  0.7 0.7 copy-start.5
  2.0 0.7 copy-start.3
  76.8 1.6 %copy-start.1 = (f32[64,4,128]{2,1,0:T(4,128)S(1)}, f32[64,4,128]{2,1,0:T(4,128)}, u32[]{:S(2)}) copy-start(f32[64,4,128]{2,1,0:T(4,128)} %get-tuple-element.10) | copy-start | bytes 393220
  77.7 2.8 %copy-start.2 = (f32[256,512]{1,0:T(8,128)S(1)}, f32[256,512]{1,0:T(8,128)}, u32[]{:S(2)}) copy-start(f32[256,512]{1,0:T(8,128)} %get-tuple-element.38) | copy-start | bytes 1572868

commit v2 on v1

v2 whole, which is shorter than its diff:
```python
import functools
import math

import jax
import jax.numpy as jnp
import numpy as np
from jax import lax
from jax.experimental import pallas as pl
from jax.experimental.pallas import tpu as pltpu
from jax.sharding import PartitionSpec as P

GROUPS = 64
PEERS = 4
NARROW = 4
LENGTH = 32768
LOCAL = LENGTH // GROUPS
ORDER = 64
BANDS = 16
EMBED = 33
A = 128
M = 256
TERMS = 2 * BANDS + 2
FACTOR = 1.0 / math.sqrt(LENGTH)
EPSILON = 1e-06
F32 = jnp.float32
BF16 = jnp.bfloat16
MESH = pl.DeviceIdType.MESH
SIN = (6.283185158626588, -10.33541366421067, 5.100061181598971, -1.19608076409451, 0.154421099195309)
COS = (0.9999999530044438, -4.934792784653484, 4.058410137182749, -1.331866894431586, 0.21966648431395203)
KK = 4
EARLY = 4
VMEM_LIMIT = 60 * 2**20


def split_np(x):
    hi = np.asarray(x, np.float32).astype(jnp.bfloat16)
    lo = (np.asarray(x, np.float64) - hi.astype(np.float64)).astype(jnp.bfloat16)
    return hi, lo


@functools.cache
def tables():
    row = np.arange(A)
    place = 2 * (row % 64) + row // 64
    k1 = np.arange(A)[:, None] + 0.25
    m = np.arange(M)
    phase = 2 * np.pi * k1 * place[None, :] / A
    first = np.concatenate([np.cos(phase), -np.sin(phase)], axis=0)
    twist = -2 * np.pi * k1 * m[None, :] / LENGTH
    grid = 2 * np.pi * (np.outer(m, m) % M) / M
    c, s = np.cos(grid), np.sin(grid)
    second = np.block([[c, -s], [s, c]])
    last = np.concatenate([np.cos(phase), -np.sin(phase)], axis=0).T / LENGTH
    out = {}
    out["t1h"], out["t1l"] = split_np(first)
    out["dh"], out["dl"] = split_np(second)
    out["t2h"], out["t2l"] = split_np(last)
    out["twr"] = np.cos(twist).astype(np.float32)
    out["twi"] = np.sin(twist).astype(np.float32)
    b = np.arange(1, BANDS + 1)
    alpha = 2 * np.pi * np.outer(place, b) / A
    beta = 2 * np.pi * np.outer(b, m) / LENGTH
    ones = np.ones((A, 1))
    ca = np.concatenate([np.cos(alpha), np.cos(alpha), place[:, None] / A, ones], axis=1)
    sa = np.concatenate([np.sin(alpha), np.sin(alpha), 0 * ones, 0 * ones], axis=1)
    q = np.concatenate([np.cos(beta), np.sin(beta), np.ones((1, M)), m[None, :] / LENGTH], axis=0)
    wide = lambda x: np.pad(np.tile(x, (1, 3)), ((0, 0), (0, 128 - 3 * TERMS))).astype(np.float32)
    out["ca"], out["sa"] = wide(ca), wide(sa)
    qh, rest = split_np(q)[0], None
    qm = (q - qh.astype(np.float64)).astype(jnp.bfloat16)
    out["q3"] = np.pad(np.concatenate([qh, qm, qh], axis=0), ((0, 128 - 3 * TERMS), (0, 0)))
    qb = np.zeros((2 * M, 128), jnp.bfloat16)
    qb[:M, :TERMS] = qh.T
    qb[:M, TERMS : 2 * TERMS] = qm.T
    qb[M:, :TERMS] = qh.T
    out["qb"] = qb
    e1 = np.zeros((TERMS, 40), np.float32)
    e2 = np.zeros((TERMS, 40), np.float32)
    for i in range(BANDS):
        e1[i, 1 + i] = 1
        e1[BANDS + i, 1 + BANDS + i] = 1
        e2[i, 1 + BANDS + i] = 1
        e2[BANDS + i, 1 + i] = -1
    e1[2 * BANDS :, 0] = 1
    out["ea"], out["eb"] = wide(e1.T), wide(e2.T)
    return out


NAMES = ("t1h", "t1l", "dh", "dl", "t2h", "t2l", "twr", "twi", "ca", "sa", "q3", "qb", "ea", "eb")


def halves(x):
    hi = x.astype(BF16)
    return hi, (x - hi.astype(F32)).astype(BF16)


def dot(a, b):
    return jnp.dot(a, b, preferred_element_type=F32)


def mm3(ah, al, bh, bl):
    return dot(ah, bh) + dot(al, bh) + dot(ah, bl)


def sin_cos(x):
    magic = 12582912.0
    f = x - ((x + magic) - magic)
    z = f * f
    s = SIN[4]
    for a in SIN[3::-1]:
        s = s * z + a
    s = s * f
    c = COS[4]
    for a in COS[3::-1]:
        c = c * z + a
    return s * c, 1.0 - (0.5 * s) * s


def kernel(comm, *refs):
    it = iter(refs)
    take = lambda n: [next(it) for _ in range(n)]
    sig_in, cot_in, first_in, second_in, rate_in, gain_in = take(6)
    t_in = dict(zip(NAMES, take(len(NAMES))))
    y_recv, gath, first_out = take(3)
    t = dict(zip(NAMES, take(len(NAMES))))
    sig, cot, weights, cols, rate, gain = take(6)
    s_send, c_send = take(2)
    s_recv, c_recv, y_send = take(2), next(it), next(it)
    basis, cosb, part, pbuf, bbuf, raw, dmix = take(7)
    xh, xl, gh, gl, spec_f, spec_c, spec_s, wbuf = take(8)
    mid, sgs, u_ref, v_ref, ug, vg, red_a, red_b, red_c = take(9)
    send_sem, recv_sem, load_sem = take(3)

    bi = lax.axis_index("batch") if comm else 0
    ci = lax.axis_index("chan") if comm else 0
    peer = lambda i: lax.rem(bi + 1 + lax.rem(i + 31, GROUPS - 1), GROUPS)
    loads = [(cot_in, cot), (sig_in, sig), (first_in, weights), (second_in, cols), (rate_in, rate), (gain_in, gain)]
    loads += [(t_in[name], t[name]) for name in NAMES]
    loads = [pltpu.make_async_copy(src, dst, load_sem.at[i]) for i, (src, dst) in enumerate(loads)]
    for load in loads[:2]:
        load.start()

    if comm:
        barrier = pltpu.get_barrier_semaphore()

        def greet(i, _):
            pl.semaphore_signal(barrier, inc=1, device_id={"batch": peer(i)}, device_id_type=MESH)
            return 0

        lax.fori_loop(0, GROUPS - 1, greet, 0)
        for i in range(1, PEERS):
            pl.semaphore_signal(barrier, inc=1, device_id={"chan": lax.rem(ci + i, PEERS)}, device_id_type=MESH)

    for load in loads[2:]:
        load.start()

    def spread(src, dst, slot, skip, step, at, to, rows=8):
        def push(i, _):
            p = peer(i)
            pltpu.make_async_remote_copy(
                src_ref=src.at[pl.ds(pl.multiple_of(p * skip + at, 8), rows)],
                dst_ref=dst.at[pl.ds(pl.multiple_of(bi * step + to, 8), rows)],
                send_sem=send_sem.at[slot],
                recv_sem=recv_sem.at[slot],
                device_id={"batch": p},
                device_id_type=MESH,
            ).start()
            return 0

        lax.fori_loop(0, GROUPS - 1, push, 0)
        own = pl.ds(pl.multiple_of(bi * step + to, 8), rows)
        dst[own, :] = src[pl.ds(pl.multiple_of(bi * skip + at, 8), rows), :]

    def landed(span, sem, slot):
        pltpu.make_async_copy(span, span, sem.at[slot]).wait()

    def arrived(buf, sem, slot):
        landed(buf.at[pl.ds(0, (GROUPS - 1) * 8)], sem, slot)

    for q in range(4 if comm else 0):
        if q == 0:
            loads[0].wait()
        c_send[pl.ds(q, 256, stride=4), :] = cot[:, q * 128 : q * 128 + 128]
    for q in range(4 if comm else 0):
        if q == 0:
            loads[1].wait()
        s_send[pl.ds(q, 256, stride=4), :] = sig[:, q * 128 : q * 128 + 128]
    if not comm:
        loads[0].wait()
        loads[1].wait()
        for h in range(2):
            for r in range(4):
                rows = pl.ds(h * 512 + r * 128, 128)
                c_recv[h * 512 + r * 128 : h * 512 + r * 128 + 128, :] = cot[rows, :]
                s_recv[h][r * 128 : r * 128 + 128, :] = sig[rows, :]
    for load in loads[2:]:
        load.wait()

    high = lax.Precision.HIGHEST
    place = bi * NARROW
    turn = (((0,), (0,)), ((), ()))
    turns = 0.5 / math.pi
    u_ref[...] = turns * lax.dot_general(weights[...], t["ea"][:EMBED], turn, precision=high, preferred_element_type=F32)
    v_ref[...] = turns * lax.dot_general(weights[...], t["eb"][:EMBED], turn, precision=high, preferred_element_type=F32)

    lane = lax.broadcasted_iota(jnp.int32, (1, 128), 1)
    raw[...] = jnp.zeros_like(raw)

    def hidden(step, _):
        for i in range(KK):
            k = step * KK + i
            for r in range(0, A, 32):
                rows = slice(r, r + 32)
                p = u_ref[pl.ds(k, 1), :] * t["ca"][rows, :] + v_ref[pl.ds(k, 1), :] * t["sa"][rows, :]
                p = jnp.where(lane < 2 * TERMS, p, p - p.astype(BF16).astype(F32))
                pbuf[i * A + r : i * A + r + 32, :] = p.astype(BF16)
        bbuf[...] = dot(pbuf[...], t["q3"][...])

        for r in range(0, A, 16):
            rows = slice(r, r + 16)
            acc = [raw[c, rows, :] for c in range(NARROW)]
            for i in range(KK):
                k = step * KK + i
                sine, cosine = sin_cos(bbuf[i * A + r : i * A + r + 16, :])
                basis[k, rows, :] = sine
                cosb[k, rows, :] = cosine
                for c in range(NARROW):
                    acc[c] = acc[c] + sine * cols[k, place + c]
            for c in range(NARROW):
                raw[c, rows, :] = acc[c]
        return 0

    lax.fori_loop(0, EARLY, hidden, 0)
    if comm:
        pl.semaphore_wait(barrier, GROUPS - 1 + PEERS - 1)
        spread(c_send, c_recv, 0, 16, 16, 0, 0, 16)
        for h in range(2):
            spread(s_send, s_recv[h], 2 + h, 16, 8, 8 * h, 0)
    lax.fori_loop(EARLY, ORDER // KK, hidden, 0)

    row = lax.broadcasted_iota(jnp.int32, (A, M), 0)
    col = lax.broadcasted_iota(jnp.int32, (A, M), 1)
    where = 512 * lax.rem(row, 64) + 256 * (row // 64) + col
    fraction = where.astype(F32) * (1.0 / LENGTH)

    def total(x):
        return jnp.sum(jnp.sum(x, axis=1, keepdims=True), axis=0, keepdims=True)

    def forward(load, spec, at, count):
        for c in range(count):
            xh[...], xl[...] = halves(load(c))
            f = mm3(t["t1h"][...], t["t1l"][...], xh[...], xl[...])
            re, im = f[:A], f[A:]
            rows = slice(c * A, c * A + A)
            gh[rows, :M], gl[rows, :M] = halves(re * t["twr"][...] - im * t["twi"][...])
            gh[rows, M:], gl[rows, M:] = halves(re * t["twi"][...] + im * t["twr"][...])
        rows = slice(0, count * A)
        spec[at * A : (at + count) * A, :] = mm3(gh[rows, :], gl[rows, :], t["dh"][...], t["dl"][...])

    def inverse(one, at, pair, store):
        for c in range(2):
            rows = slice(c * A, c * A + A)
            from_one = slice((at + c) * A, (at + c + 1) * A)
            from_two = slice((2 * pair + c) * A, (2 * pair + c + 1) * A)
            r1, i1 = one[from_one, :M], one[from_one, M:]
            r2, i2 = spec_c[from_two, :M], spec_c[from_two, M:]
            gh[rows, :M], gl[rows, :M] = halves(r1 * r2 + i1 * i2)
            gh[rows, M:], gl[rows, M:] = halves(r1 * i2 - i1 * r2)
        rows = slice(0, 2 * A)
        across = (((1,), (1,)), ((), ()))
        tdot = lambda a, b: lax.dot_general(a, b, across, preferred_element_type=F32)
        high_part, low_part = gh[rows, :], gl[rows, :]
        wbuf[...] = (
            tdot(high_part, t["dh"][...]) + tdot(low_part, t["dh"][...]) + tdot(high_part, t["dl"][...])
        )
        for c in range(2):
            rows = slice(c * A, c * A + A)
            re, im = wbuf[rows, :M], wbuf[rows, M:]
            mid[:A, :] = re * t["twr"][...] + im * t["twi"][...]
            mid[A:, :] = im * t["twr"][...] - re * t["twi"][...]
            h, low = halves(mid[...])
            store(c, mm3(t["t2h"][...], t["t2l"][...], h, low))

    def blocks_of(buf, c, stride):
        parts = [[buf[pl.ds(4 * c + 2 * h + q, 64, stride=stride), :] for q in range(2)] for h in range(2)]
        return jnp.concatenate([jnp.concatenate(p, axis=1) for p in parts], axis=0)

    norms = []
    for c in range(NARROW):
        value = raw[c] * jnp.exp(-rate[place + c] * fraction)
        raw[c] = value
        norms.append(jnp.sqrt(total(value * value) + EPSILON))
    forward(lambda c: raw[c] / norms[c], spec_f, 0, NARROW)
    sgs[...] = jnp.zeros_like(sgs)

    def store_grad(c, y):
        y = y + gain[place + c] * blocks_of(c_recv, c, 16)
        for h in range(2):
            for q in range(2):
                y_send[pl.ds(4 * c + 2 * h + q, 64, stride=16), :] = y[h * 64 : h * 64 + 64, q * 128 : q * 128 + 128]

    if comm:
        landed(c_recv.at[pl.ds(0, (GROUPS - 1) * 16)], recv_sem, 0)
    forward(lambda c: blocks_of(c_recv, c, 16), spec_c, 0, NARROW)
    for pair in range(2):
        inverse(spec_f, 2 * pair, pair, lambda c, y: store_grad(2 * pair + c, y))
    if comm:
        spread(y_send, y_recv, 4, 16, 16, 0, 0, 16)
    else:
        for r in range(8):
            y_recv[r * 128 : r * 128 + 128, :] = y_send[r * 128 : r * 128 + 128, :]

    def filter_grad(pair):
        if comm:
            arrived(s_recv[pair], recv_sem, 2 + pair)
        forward(lambda c: blocks_of(s_recv[pair], c, 8), spec_s, 0, 2)

        def store(c, y):
            ch = 2 * pair + c
            dfilt = FACTOR * y
            norm = norms[ch]
            value = raw[ch]
            filt = value / norm
            project = total(filt * dfilt)
            draw = (dfilt - filt * project) / norm
            decay = -jnp.sum(draw * value * fraction, axis=0, keepdims=True)
            skip = blocks_of(c_recv, ch, 16) * blocks_of(s_recv[pair], c, 8)
            skip = FACTOR * jnp.sum(skip, axis=0, keepdims=True)
            sgs[ch * 128 + 64 : ch * 128 + 65, :] = decay[:, :128] + decay[:, 128:]
            sgs[ch * 128 + 65 : ch * 128 + 66, :] = skip[:, :128] + skip[:, 128:]
            dmix[ch] = draw * jnp.exp(-rate[place + ch] * fraction)

        inverse(spec_s, 0, pair, store)

    def half_back(step, _):
        for r in range(0, A, 16):
            rows = slice(r, r + 16)
            d = [dmix[c, rows, :] for c in range(2)]
            for i in range(KK):
                k = step * KK + i
                part[k, rows, :] = d[0] * cols[k, place] + d[1] * cols[k, place + 1]
        return 0

    def fill(buf, step):
        for r in range(0, A, 16):
            rows = slice(r, r + 16)
            d = [dmix[c, rows, :] for c in range(2, 4)]
            for i in range(KK):
                k = step * KK + i
                g = part[k, rows, :] + d[0] * cols[k, place + 2] + d[1] * cols[k, place + 3]
                ghi, glo = halves(g * cosb[k, rows, :])
                buf[i * A + r : i * A + r + 16, :M] = ghi
                buf[i * A + r : i * A + r + 16, M:] = glo

    def contract(buf, step):
        hmat = dot(buf[...], t["qb"][...])
        for i in range(KK):
            h = hmat[i * A : i * A + A]
            at = pl.ds(step * KK + i + 8, 1)
            ug[at, :] = jnp.sum(h * t["ca"][...], axis=0, keepdims=True)
            vg[at, :] = jnp.sum(h * t["sa"][...], axis=0, keepdims=True)

    def first_back(two, _):
        fill(gh, 2 * two)
        contract(gl, 2 * two - 1)
        fill(gl, 2 * two + 1)
        contract(gh, 2 * two)
        return 0

    def second_back(step, _):
        sums = [[jnp.zeros((8, 128), F32) for _ in range(NARROW)] for _ in range(KK)]
        for r in range(0, A, 16):
            rows = slice(r, r + 16)
            d = [dmix[c, rows, :] for c in range(NARROW)]
            for i in range(KK):
                b = basis[step * KK + i, rows, :]
                for c in range(NARROW):
                    e = b * d[c]
                    sums[i][c] = sums[i][c] + ((e[:8, :128] + e[:8, 128:]) + (e[8:, :128] + e[8:, 128:]))
        for i in range(KK):
            for c in range(NARROW):
                sgs[pl.ds(c * 128 + step * KK + i, 1), :] = jnp.sum(sums[i][c], axis=0, keepdims=True)
        return 0

    filter_grad(0)
    lax.fori_loop(0, ORDER // KK, half_back, 0)
    filter_grad(1)
    lax.fori_loop(0, ORDER // KK // 2, first_back, 0)
    contract(gl, ORDER // KK - 1)

    across = (((1,), (1,)), ((), ()))
    hdot = lambda a, b: lax.dot_general(a, b, across, precision=high, preferred_element_type=F32)
    lanes = lax.broadcasted_iota(jnp.int32, (1, 128), 1)
    two = lambda x: jnp.where(lanes < 2 * TERMS, x, 0.0)
    first = hdot(two(t["ea"][...]), ug[8:, :]) + hdot(two(t["eb"][...]), vg[8:, :])
    first = jnp.concatenate(
        [
            jnp.concatenate([first[:16], first[16:32]], axis=1),
            jnp.concatenate([first[32:40], jnp.zeros((8, 64), F32)], axis=1),
        ],
        axis=0,
    )

    def issue(buf, slot, value, me, count, target):
        buf[pl.ds(me, 1)] = value[None]
        for i in range(1, count):
            pltpu.make_async_remote_copy(
                src_ref=buf.at[me],
                dst_ref=buf.at[me],
                send_sem=send_sem.at[slot],
                recv_sem=recv_sem.at[slot],
                device_id=target(lax.rem(me + i, count)),
                device_id_type=MESH,
            ).start()

    def collect(buf, slot, count):
        landed(buf.at[pl.ds(0, count - 1)], recv_sem, slot)
        value = buf[0]
        for i in range(1, count):
            value = value + buf[i]
        return value

    if comm:
        issue(red_a, 7, first, ci, PEERS, lambda p: {"chan": p})

    lax.fori_loop(0, ORDER // KK, second_back, 0)
    ones = jnp.ones((8, 128), F32)
    block = jnp.concatenate([hdot(ones, sgs[c * 128 : c * 128 + 128, :])[:1] for c in range(NARROW)], axis=0)

    if not comm:
        gath[...] = jnp.zeros_like(gath)
        gath[0] = block
        first_out[...] = first
        return

    def tell(i, _):
        pltpu.make_async_remote_copy(
            src_ref=gath.at[bi],
            dst_ref=gath.at[bi],
            send_sem=send_sem.at[6],
            recv_sem=recv_sem.at[6],
            device_id={"batch": peer(i)},
            device_id_type=MESH,
        ).start()
        return 0

    zi, xy = bi // 8, lax.rem(bi, 8)
    first = collect(red_a, 7, PEERS)
    issue(red_c, 8, first, xy, 8, lambda p: {"batch": zi * 8 + p})
    gath[pl.ds(bi, 1)] = block[None]
    lax.fori_loop(0, GROUPS - 1, tell, 0)
    first = collect(red_c, 8, 8)
    issue(red_b, 9, first, zi, 8, lambda p: {"batch": p * 8 + xy})
    first_out[...] = collect(red_b, 9, 8)

    whole = y_recv.at[pl.ds(0, (GROUPS - 1) * 16)]
    landed(whole, recv_sem, 4)
    landed(gath.at[pl.ds(0, GROUPS - 1)], recv_sem, 6)
    for slot in (0, 4):
        landed(whole, send_sem, slot)
    for slot in (2, 3):
        arrived(y_recv, send_sem, slot)
    landed(gath.at[pl.ds(0, GROUPS - 1)], send_sem, 6)
    landed(red_a.at[pl.ds(0, PEERS - 1)], send_sem, 7)
    landed(red_c.at[pl.ds(0, 7)], send_sem, 8)
    landed(red_b.at[pl.ds(0, 7)], send_sem, 9)


def finish(y, gath, first, grad, first_grad, second_grad, decay_grad, skip_grad):
    for q in range(4):
        grad[:, q * 128 : q * 128 + 128] = y[pl.ds(q, 256, stride=4), :]
    turned = gath[...].T
    second_grad[...] = turned[:ORDER]
    decay_grad[...] = turned[ORDER : ORDER + 1]
    skip_grad[...] = turned[ORDER + 1 : ORDER + 2]
    first_grad[:16] = first[:16, :ORDER]
    first_grad[16:32] = first[:16, ORDER:]
    first_grad[32:33] = first[16:17, :ORDER]


def call(comm, sig, cot, first_layer, second_layer, rate, gain):
    vmem = pl.BlockSpec(memory_space=pltpu.VMEM)
    anywhere = pl.BlockSpec(memory_space=pl.ANY)
    t = tables()
    line = lambda: pltpu.VMEM((GROUPS * 16, 128), F32)
    half = lambda: pltpu.VMEM((GROUPS * 8, 128), F32)
    scratch = [pltpu.VMEM(t[name].shape, t[name].dtype) for name in NAMES]
    scratch += [
        pltpu.VMEM(sig.shape, F32),
        pltpu.VMEM(cot.shape, F32),
        pltpu.VMEM(first_layer.shape, F32),
        pltpu.SMEM(second_layer.shape, F32),
        pltpu.SMEM(rate.shape, F32),
        pltpu.SMEM(gain.shape, F32),
        line(),
        line(),
    ]
    scratch += [half(), half(), line(), line()]
    scratch += [
        pltpu.VMEM((ORDER, A, M), F32),
        pltpu.VMEM((ORDER, A, M), F32),
        pltpu.VMEM((ORDER, A, M), F32),
        pltpu.VMEM((KK * A, 128), BF16),
        pltpu.VMEM((KK * A, M), F32),
        pltpu.VMEM((NARROW, A, M), F32),
        pltpu.VMEM((NARROW, A, M), F32),
        pltpu.VMEM((A, M), BF16),
        pltpu.VMEM((A, M), BF16),
        pltpu.VMEM((NARROW * A, 2 * M), BF16),
        pltpu.VMEM((NARROW * A, 2 * M), BF16),
        pltpu.VMEM((NARROW * A, 2 * M), F32),
        pltpu.VMEM((NARROW * A, 2 * M), F32),
        pltpu.VMEM((2 * A, 2 * M), F32),
        pltpu.VMEM((2 * A, 2 * M), F32),
        pltpu.VMEM((2 * A, M), F32),
        pltpu.VMEM((NARROW * 128, 128), F32),
        pltpu.VMEM((ORDER, 128), F32),
        pltpu.VMEM((ORDER, 128), F32),
        pltpu.VMEM((ORDER + 8, 128), F32),
        pltpu.VMEM((ORDER + 8, 128), F32),
        pltpu.VMEM((PEERS, 24, 128), F32),
        pltpu.VMEM((8, 24, 128), F32),
        pltpu.VMEM((8, 24, 128), F32),
        pltpu.SemaphoreType.DMA((10,)),
        pltpu.SemaphoreType.DMA((10,)),
        pltpu.SemaphoreType.DMA((6 + len(NAMES),)),
    ]
    params = dict(vmem_limit_bytes=VMEM_LIMIT)
    if comm:
        params.update(collective_id=0, has_side_effects=True)
    return pl.pallas_call(
        functools.partial(kernel, comm),
        out_shape=(
            jax.ShapeDtypeStruct((GROUPS * 16, 128), F32),
            jax.ShapeDtypeStruct((GROUPS, NARROW, 128), F32),
            jax.ShapeDtypeStruct((24, 128), F32),
        ),
        in_specs=[anywhere] * (6 + len(NAMES)),
        out_specs=(vmem, vmem, vmem),
        scratch_shapes=scratch,
        compiler_params=pltpu.CompilerParams(**params),
        name="hyena_back",
    )(sig, cot, first_layer, second_layer, rate, gain, *[jnp.asarray(t[name]) for name in NAMES])


def local(signal, cotangent, first_layer, second_layer, decay_rate, skip_gain):
    y, gath, first = call(True, signal, cotangent, first_layer, second_layer, decay_rate, skip_gain)
    vmem = pl.BlockSpec(memory_space=pltpu.VMEM)
    grad, first_grad, second_grad, decay_grad, skip_grad = pl.pallas_call(
        finish,
        out_shape=(
            jax.ShapeDtypeStruct(signal.shape, F32),
            jax.ShapeDtypeStruct(first_layer.shape, F32),
            jax.ShapeDtypeStruct(second_layer.shape, F32),
            jax.ShapeDtypeStruct((1, decay_rate.shape[0]), F32),
            jax.ShapeDtypeStruct((1, skip_gain.shape[0]), F32),
        ),
        in_specs=[vmem] * 3,
        out_specs=(vmem,) * 5,
        name="finish",
    )(y, gath.reshape(GROUPS * NARROW, 128), first)
    return grad, first_grad, second_grad, decay_grad.reshape(-1), skip_grad.reshape(-1)


def solution(mesh):
    placed = (P("chan", "batch"), P("chan", "batch"), P(), P(None, "chan"), P("chan"), P("chan"))
    return jax.shard_map(
        local,
        mesh=mesh,
        in_specs=placed,
        out_specs=(P("chan", "batch"), P(), P(None, "chan"), P("chan"), P("chan")),
        check_vma=False,
    )
```

time: 81.6 us -> 67.6 us (0.83)
  local copies, waits for them, and re-layouts: 7.47 us -> 0 us
  Pallas kernels: 72.5 us -> 66.7 us
    pallas_call x1, Pallas kernels: 72.5 us -> 64.7 us  [call(): pl.pallas_call(functools.partial(kernel, comm), out_shape=(jax.ShapeDtype...]
    unnamed x17 -> x0, local copies, waits for them, and re-layouts: 4.25 us -> none
    pallas_call x0 -> x1, Pallas kernels: none -> 2 us  [local(): pl.pallas_call(finish, out_shape=(jax.ShapeDtypeStruct(signal.shape, F32)...]
    pad x2 -> x0, local copies, waits for them, and re-layouts: 1.27 us -> none  [terms(): jnp.pad(jnp.tile(x, (1, 6)), ((0, 0), (0, 256 - 6 * TERMS)))]
    slice x3 -> x0, local copies, waits for them, and re-layouts: 0.99 us -> none  [the longest x1 0.87 us: local(): first[:, :EMBED]]
where the time goes in v2:
time: 67.6 us; the launch traced here: 67.3 us
  Pallas kernels  66.7 us (99%)
    pallas_call x1, Pallas kernels, call(): pl.pallas_call(functools.partial(kernel, comm), out_shape=(jax.ShapeDtype...  64.7 us
    pallas_call x1, Pallas kernels, local(): pl.pallas_call(finish, out_shape=(jax.ShapeDtypeStruct(signal.shape, F32)...  2 us

profile of v2, /device:TPU:1, one launch (start us, length us, event | category | flops | bytes accessed | tf_op | source)
XLA Modules:
  0.0 67.3 jit_solution(1907842448472584133)
XLA Ops:
  0.6 64.7 %hyena_back.1 = (f32[1024,128]{1,0:T(8,128)}, f32[64,4,128]{2,1,0:T(4,128)}, f32[24,128]{1,0:T(8,128)}) custom-call(f32[256,512]{1,0:T(8,128)} %refs_0_.1, f32[256,512]{1,0:T(8,128)} %refs_1_.1, f32[33,64]{1,0:T(8,128)} %refs_2_.1, f32[64,256]{1,0:T(8,128)} %refs_3_.1, f32[256]{0:T(256)} %refs_4_.1, f32[256]{0:T(256)} %refs_5_.1, ...), custom_call_target="tpu_custom_call" | custom-call | tf_op jit(solution)/shard_map/hyena_back/pallas_call | solution.py:531
  65.3 2.0 %finish.1 = (f32[256,512]{1,0:T(8,128)}, f32[33,64]{1,0:T(8,128)}, f32[64,256]{1,0:T(8,128)}, f32[1,256]{1,0:T(1,128)}, f32[1,256]{1,0:T(1,128)}) custom-call(f32[1024,128]{1,0:T(8,128)} %get-tuple-element.13.y, f32[256,128]{1,0:T(8,128)} %bitcast.3, f32[24,128]{1,0:T(8,128)} %get-tuple-element.15.first), custom_call_target="tpu_custom_call" | custom-call | tf_op jit(solution)/shard_map/finish/pallas_call | solution.py:549

commit v3 on v2

--- a/solution.py
+++ b/solution.py
@@ -28,8 +28,10 @@
 SIN = (6.283185158626588, -10.33541366421067, 5.100061181598971, -1.19608076409451, 0.154421099195309)
 COS = (0.9999999530044438, -4.934792784653484, 4.058410137182749, -1.331866894431586, 0.21966648431395203)
 KK = 4
-EARLY = 4
-VMEM_LIMIT = 60 * 2**20
+EARLY = 3
+VMEM_LIMIT = 66300000
+OUT = pltpu.VMEM
+PIN = False
 
 
 def split_np(x):
@@ -121,7 +123,10 @@
     take = lambda n: [next(it) for _ in range(n)]
     sig_in, cot_in, first_in, second_in, rate_in, gain_in = take(6)
     t_in = dict(zip(NAMES, take(len(NAMES))))
-    y_recv, gath, first_out = take(3)
+    if comm:
+        grad, first_grad, second_grad, decay_grad, skip_grad = take(5)
+    else:
+        y_recv, gath, first_out = take(3)
     t = dict(zip(NAMES, take(len(NAMES))))
     sig, cot, weights, cols, rate, gain = take(6)
     s_send, c_send = take(2)
@@ -130,10 +135,20 @@
     xh, xl, gh, gl, spec_f, spec_c, spec_s, wbuf = take(8)
     mid, sgs, u_ref, v_ref, ug, vg, red_a, red_b, red_c = take(9)
     send_sem, recv_sem, load_sem = take(3)
+    if comm:
+        y_recv, gath_z, gath = take(3)
 
     bi = lax.axis_index("batch") if comm else 0
     ci = lax.axis_index("chan") if comm else 0
-    peer = lambda i: lax.rem(bi + 1 + lax.rem(i + 31, GROUPS - 1), GROUPS)
+
+    def others(visit):
+        def step(i, _):
+            visit(lax.rem(bi + i, GROUPS))
+            return 0
+
+        lax.fori_loop(GROUPS // 2, GROUPS, step, 0)
+        lax.fori_loop(1, GROUPS // 2, step, 0)
+
     loads = [(cot_in, cot), (sig_in, sig), (first_in, weights), (second_in, cols), (rate_in, rate), (gain_in, gain)]
     loads += [(t_in[name], t[name]) for name in NAMES]
     loads = [pltpu.make_async_copy(src, dst, load_sem.at[i]) for i, (src, dst) in enumerate(loads)]
@@ -143,11 +158,7 @@
     if comm:
         barrier = pltpu.get_barrier_semaphore()
 
-        def greet(i, _):
-            pl.semaphore_signal(barrier, inc=1, device_id={"batch": peer(i)}, device_id_type=MESH)
-            return 0
-
-        lax.fori_loop(0, GROUPS - 1, greet, 0)
+        others(lambda p: pl.semaphore_signal(barrier, inc=1, device_id={"batch": p}, device_id_type=MESH))
         for i in range(1, PEERS):
             pl.semaphore_signal(barrier, inc=1, device_id={"chan": lax.rem(ci + i, PEERS)}, device_id_type=MESH)
 
@@ -155,8 +166,7 @@
         load.start()
 
     def spread(src, dst, slot, skip, step, at, to, rows=8):
-        def push(i, _):
-            p = peer(i)
+        def push(p):
             pltpu.make_async_remote_copy(
                 src_ref=src.at[pl.ds(pl.multiple_of(p * skip + at, 8), rows)],
                 dst_ref=dst.at[pl.ds(pl.multiple_of(bi * step + to, 8), rows)],
@@ -165,9 +175,8 @@
                 device_id={"batch": p},
                 device_id_type=MESH,
             ).start()
-            return 0
-
-        lax.fori_loop(0, GROUPS - 1, push, 0)
+
+        others(push)
         own = pl.ds(pl.multiple_of(bi * step + to, 8), rows)
         dst[own, :] = src[pl.ds(pl.multiple_of(bi * skip + at, 8), rows), :]
 
@@ -367,23 +376,25 @@
         contract(gh, 2 * two)
         return 0
 
-    def second_back(step, _):
-        sums = [[jnp.zeros((8, 128), F32) for _ in range(NARROW)] for _ in range(KK)]
+    def second_back(pair, step, _):
+        sums = [[jnp.zeros((8, 128), F32) for _ in range(2)] for _ in range(KK)]
         for r in range(0, A, 16):
             rows = slice(r, r + 16)
-            d = [dmix[c, rows, :] for c in range(NARROW)]
+            d = [dmix[2 * pair + c, rows, :] for c in range(2)]
             for i in range(KK):
                 b = basis[step * KK + i, rows, :]
-                for c in range(NARROW):
+                for c in range(2):
                     e = b * d[c]
                     sums[i][c] = sums[i][c] + ((e[:8, :128] + e[:8, 128:]) + (e[8:, :128] + e[8:, 128:]))
         for i in range(KK):
-            for c in range(NARROW):
-                sgs[pl.ds(c * 128 + step * KK + i, 1), :] = jnp.sum(sums[i][c], axis=0, keepdims=True)
+            for c in range(2):
+                at = (2 * pair + c) * 128 + step * KK + i
+                sgs[pl.ds(at, 1), :] = jnp.sum(sums[i][c], axis=0, keepdims=True)
         return 0
 
     filter_grad(0)
     lax.fori_loop(0, ORDER // KK, half_back, 0)
+    lax.fori_loop(0, ORDER // KK, functools.partial(second_back, 0), 0)
     filter_grad(1)
     lax.fori_loop(0, ORDER // KK // 2, first_back, 0)
     contract(gl, ORDER // KK - 1)
@@ -396,7 +407,7 @@
     first = jnp.concatenate(
         [
             jnp.concatenate([first[:16], first[16:32]], axis=1),
-            jnp.concatenate([first[32:40], jnp.zeros((8, 64), F32)], axis=1),
+            jnp.concatenate([first[32:33], jnp.zeros((1, 64), F32)], axis=1),
         ],
         axis=0,
     )
@@ -423,7 +434,7 @@
     if comm:
         issue(red_a, 7, first, ci, PEERS, lambda p: {"chan": p})
 
-    lax.fori_loop(0, ORDER // KK, second_back, 0)
+    lax.fori_loop(0, ORDER // KK, functools.partial(second_back, 1), 0)
     ones = jnp.ones((8, 128), F32)
     block = jnp.concatenate([hdot(ones, sgs[c * 128 : c * 128 + 128, :])[:1] for c in range(NARROW)], axis=0)
 
@@ -433,54 +444,55 @@
         first_out[...] = first
         return
 
-    def tell(i, _):
-        pltpu.make_async_remote_copy(
-            src_ref=gath.at[bi],
-            dst_ref=gath.at[bi],
-            send_sem=send_sem.at[6],
-            recv_sem=recv_sem.at[6],
-            device_id={"batch": peer(i)},
-            device_id_type=MESH,
-        ).start()
-        return 0
-
     zi, xy = bi // 8, lax.rem(bi, 8)
+    along_z = lambda p: {"batch": p * 8 + xy}
+    in_plane = lambda p: {"batch": zi * 8 + p}
+    issue(gath_z, 5, block, zi, 8, along_z)
     first = collect(red_a, 7, PEERS)
-    issue(red_c, 8, first, xy, 8, lambda p: {"batch": zi * 8 + p})
-    gath[pl.ds(bi, 1)] = block[None]
-    lax.fori_loop(0, GROUPS - 1, tell, 0)
+    issue(red_c, 8, first, xy, 8, in_plane)
+    landed(gath_z.at[pl.ds(0, 7)], recv_sem, 5)
+    issue(gath, 6, gath_z[...], xy, 8, in_plane)
     first = collect(red_c, 8, 8)
-    issue(red_b, 9, first, zi, 8, lambda p: {"batch": p * 8 + xy})
-    first_out[...] = collect(red_b, 9, 8)
+    issue(red_b, 9, first, zi, 8, along_z)
 
     whole = y_recv.at[pl.ds(0, (GROUPS - 1) * 16)]
     landed(whole, recv_sem, 4)
-    landed(gath.at[pl.ds(0, GROUPS - 1)], recv_sem, 6)
+    for q in range(4):
+        grad[:, q * 128 : q * 128 + 128] = y_recv[pl.ds(q, 256, stride=4), :]
+    landed(gath.at[pl.ds(0, 7)], recv_sem, 6)
+    every = jnp.concatenate([gath[:, z].reshape(8 * NARROW, 128) for z in range(8)], axis=0)
+    turned = every.T
+    second_grad[...] = turned[:ORDER]
+    decay_grad[...] = turned[ORDER : ORDER + 1]
+    skip_grad[...] = turned[ORDER + 1 : ORDER + 2]
+    first = collect(red_b, 9, 8)
+    first_grad[:16] = first[:16, :ORDER]
+    first_grad[16:32] = first[:16, ORDER:]
+    first_grad[32:33] = first[16:17, :ORDER]
+
     for slot in (0, 4):
         landed(whole, send_sem, slot)
     for slot in (2, 3):
         arrived(y_recv, send_sem, slot)
-    landed(gath.at[pl.ds(0, GROUPS - 1)], send_sem, 6)
+    landed(gath_z.at[pl.ds(0, 7)], send_sem, 5)
+    landed(gath.at[pl.ds(0, 7)], send_sem, 6)
     landed(red_a.at[pl.ds(0, PEERS - 1)], send_sem, 7)
     landed(red_c.at[pl.ds(0, 7)], send_sem, 8)
     landed(red_b.at[pl.ds(0, 7)], send_sem, 9)
 
 
-def finish(y, gath, first, grad, first_grad, second_grad, decay_grad, skip_grad):
-    for q in range(4):
-        grad[:, q * 128 : q * 128 + 128] = y[pl.ds(q, 256, stride=4), :]
-    turned = gath[...].T
-    second_grad[...] = turned[:ORDER]
-    decay_grad[...] = turned[ORDER : ORDER + 1]
-    skip_grad[...] = turned[ORDER + 1 : ORDER + 2]
-    first_grad[:16] = first[:16, :ORDER]
-    first_grad[16:32] = first[:16, ORDER:]
-    first_grad[32:33] = first[16:17, :ORDER]
+def finish(*refs):
+    sem = refs[10]
+    copies = [pltpu.make_async_copy(refs[i], refs[5 + i], sem.at[i]) for i in range(5)]
+    for copy in copies:
+        copy.start()
+    for copy in copies:
+        copy.wait()
 
 
 def call(comm, sig, cot, first_layer, second_layer, rate, gain):
     vmem = pl.BlockSpec(memory_space=pltpu.VMEM)
-    anywhere = pl.BlockSpec(memory_space=pl.ANY)
+    anywhere = pl.BlockSpec(memory_space=pltpu.HBM)
     t = tables()
     line = lambda: pltpu.VMEM((GROUPS * 16, 128), F32)
     half = lambda: pltpu.VMEM((GROUPS * 8, 128), F32)
@@ -518,47 +530,47 @@
         pltpu.VMEM((ORDER, 128), F32),
         pltpu.VMEM((ORDER + 8, 128), F32),
         pltpu.VMEM((ORDER + 8, 128), F32),
-        pltpu.VMEM((PEERS, 24, 128), F32),
-        pltpu.VMEM((8, 24, 128), F32),
-        pltpu.VMEM((8, 24, 128), F32),
+        pltpu.VMEM((PEERS, 17, 128), F32),
+        pltpu.VMEM((8, 17, 128), F32),
+        pltpu.VMEM((8, 17, 128), F32),
         pltpu.SemaphoreType.DMA((10,)),
         pltpu.SemaphoreType.DMA((10,)),
         pltpu.SemaphoreType.DMA((6 + len(NAMES),)),
     ]
     params = dict(vmem_limit_bytes=VMEM_LIMIT)
-    if comm:
+    shapes = out_shapes(sig, first_layer, second_layer, rate, gain)
+    if comm:
+        scratch += [line(), pltpu.VMEM((8, NARROW, 128), F32), pltpu.VMEM((8, 8, NARROW, 128), F32)]
         params.update(collective_id=0, has_side_effects=True)
     return pl.pallas_call(
         functools.partial(kernel, comm),
-        out_shape=(
-            jax.ShapeDtypeStruct((GROUPS * 16, 128), F32),
-            jax.ShapeDtypeStruct((GROUPS, NARROW, 128), F32),
-            jax.ShapeDtypeStruct((24, 128), F32),
+        out_shape=tuple(OUT(shape, F32) for shape in shapes) if comm else tuple(
+            jax.ShapeDtypeStruct(shape, F32) for shape in ((GROUPS * 16, 128), (GROUPS, NARROW, 128), (17, 128))
         ),
         in_specs=[anywhere] * (6 + len(NAMES)),
-        out_specs=(vmem, vmem, vmem),
+        out_specs=(vmem,) * (5 if comm else 3),
         scratch_shapes=scratch,
         compiler_params=pltpu.CompilerParams(**params),
         name="hyena_back",
     )(sig, cot, first_layer, second_layer, rate, gain, *[jnp.asarray(t[name]) for name in NAMES])
 
 
+def out_shapes(sig, first_layer, second_layer, rate, gain):
+    return sig.shape, first_layer.shape, second_layer.shape, (1, rate.shape[0]), (1, gain.shape[0])
+
+
 def local(signal, cotangent, first_layer, second_layer, decay_rate, skip_gain):
-    y, gath, first = call(True, signal, cotangent, first_layer, second_layer, decay_rate, skip_gain)
-    vmem = pl.BlockSpec(memory_space=pltpu.VMEM)
+    held = call(True, signal, cotangent, first_layer, second_layer, decay_rate, skip_gain)
+    shapes = out_shapes(signal, first_layer, second_layer, decay_rate, skip_gain)
     grad, first_grad, second_grad, decay_grad, skip_grad = pl.pallas_call(
         finish,
-        out_shape=(
-            jax.ShapeDtypeStruct(signal.shape, F32),
-            jax.ShapeDtypeStruct(first_layer.shape, F32),
-            jax.ShapeDtypeStruct(second_layer.shape, F32),
-            jax.ShapeDtypeStruct((1, decay_rate.shape[0]), F32),
-            jax.ShapeDtypeStruct((1, skip_gain.shape[0]), F32),
-        ),
-        in_specs=[vmem] * 3,
-        out_specs=(vmem,) * 5,
+        out_shape=tuple(jax.ShapeDtypeStruct(shape, F32) for shape in shapes),
+        in_specs=[pl.BlockSpec(memory_space=pltpu.VMEM if PIN else pl.ANY)] * 5,
+        out_specs=(pl.BlockSpec(memory_space=pl.ANY),) * 5,
+        scratch_shapes=[pltpu.SemaphoreType.DMA((5,))],
+        compiler_params=pltpu.CompilerParams(vmem_limit_bytes=4 * 2**20),
         name="finish",
-    )(y, gath.reshape(GROUPS * NARROW, 128), first)
+    )(*held)
     return grad, first_grad, second_grad, decay_grad.reshape(-1), skip_grad.reshape(-1)
 
 

time: 67.6 us -> 64.8 us (0.959)
  Pallas kernels: 66.7 us -> 64 us
    pallas_call x2, Pallas kernels: 66.7 us -> 64 us  [the longest x1 63.2 us: call(): pl.pallas_call(functools.partial(kernel, comm), out_shape=tuple((OUT(shap...]
where the time goes in v3:
time: 64.8 us; the launch traced here: 64.7 us
  Pallas kernels  64 us (99%)
    pallas_call x1, Pallas kernels, call(): pl.pallas_call(functools.partial(kernel, comm), out_shape=tuple((OUT(shap...  63.2 us

profile of v3, /device:TPU:1, one launch (start us, length us, event | category | flops | bytes accessed | tf_op | source)
XLA Modules:
  0.0 64.7 jit_solution(6135879527616596288)
XLA Ops:
  0.6 63.2 %hyena_back.1 = (f32[256,512]{1,0:T(8,128)S(1)}, f32[33,64]{1,0:T(8,128)S(1)}, f32[64,256]{1,0:T(8,128)S(1)}, f32[1,256]{1,0:T(1,128)S(1)}, f32[1,256]{1,0:T(1,128)S(1)}) custom-call(f32[256,512]{1,0:T(8,128)} %refs_0_.1, f32[256,512]{1,0:T(8,128)} %refs_1_.1, f32[33,64]{1,0:T(8,128)} %refs_2_.1, f32[64,256]{1,0:T(8,128)} %refs_3_.1, f32[256]{0:T(256)} %refs_4_.1, ...), custom_call_target="tpu_custom_call" | custom-call | tf_op jit(solution)/shard_map/hyena_back/pallas_call | solution.py:545
  63.8 0.9 %finish.1 = (f32[256,512]{1,0:T(8,128)}, f32[33,64]{1,0:T(8,128)}, f32[64,256]{1,0:T(8,128)}, f32[1,256]{1,0:T(1,128)}, f32[1,256]{1,0:T(1,128)}) custom-call(f32[256,512]{1,0:T(8,128)S(1)} %get-tuple-element.15.refs_0_, f32[33,64]{1,0:T(8,128)S(1)} %get-tuple-element.16.refs_1_, f32[64,256]{1,0:T(8,128)S(1)} %get-tuple-element.17.refs_2_, ...), custom_call_target="tpu_custom_call" | custom-call | tf_op jit(solution)/shard_map/finish/pallas_call | solution.py:565

commit v4 on v3

--- a/solution.py
+++ b/solution.py
@@ -161,6 +161,8 @@
         others(lambda p: pl.semaphore_signal(barrier, inc=1, device_id={"batch": p}, device_id_type=MESH))
         for i in range(1, PEERS):
             pl.semaphore_signal(barrier, inc=1, device_id={"chan": lax.rem(ci + i, PEERS)}, device_id_type=MESH)
+            across_y = {"batch": bi + 1 - 2 * lax.rem(bi, 2), "chan": lax.rem(ci + i, PEERS)}
+            pl.semaphore_signal(barrier, inc=1, device_id=across_y, device_id_type=MESH)
 
     for load in loads[2:]:
         load.start()
@@ -241,7 +243,7 @@
 
     lax.fori_loop(0, EARLY, hidden, 0)
     if comm:
-        pl.semaphore_wait(barrier, GROUPS - 1 + PEERS - 1)
+        pl.semaphore_wait(barrier, GROUPS - 1 + 2 * (PEERS - 1))
         spread(c_send, c_recv, 0, 16, 16, 0, 0, 16)
         for h in range(2):
             spread(s_send, s_recv[h], 2 + h, 16, 8, 8 * h, 0)
@@ -403,7 +405,13 @@
     hdot = lambda a, b: lax.dot_general(a, b, across, precision=high, preferred_element_type=F32)
     lanes = lax.broadcasted_iota(jnp.int32, (1, 128), 1)
     two = lambda x: jnp.where(lanes < 2 * TERMS, x, 0.0)
-    first = hdot(two(t["ea"][...]), ug[8:, :]) + hdot(two(t["eb"][...]), vg[8:, :])
+    picks = jnp.concatenate([two(t["ea"][...]), two(t["eb"][...])], axis=1).astype(BF16)
+    rest = jnp.concatenate([ug[8:, :], vg[8:, :]], axis=1)
+    first = jnp.zeros((40, ORDER), F32)
+    for _ in range(3):
+        piece = rest.astype(BF16)
+        rest = rest - piece.astype(F32)
+        first = first + lax.dot_general(picks, piece, across, preferred_element_type=F32)
     first = jnp.concatenate(
         [
             jnp.concatenate([first[:16], first[16:32]], axis=1),
@@ -431,8 +439,13 @@
             value = value + buf[i]
         return value
 
-    if comm:
-        issue(red_a, 7, first, ci, PEERS, lambda p: {"chan": p})
+    zi, xi, yi, xy = bi // 8, lax.rem(bi // 2, 4), lax.rem(bi, 2), lax.rem(bi, 8)
+    along_y = lambda p: {"batch": bi - yi + p // PEERS, "chan": lax.rem(p, PEERS)}
+    along_x = lambda p: {"batch": zi * 8 + p * 2 + yi}
+    along_z = lambda p: {"batch": p * 8 + xy}
+    in_plane = lambda p: {"batch": zi * 8 + p}
+    if comm:
+        issue(red_a, 7, first, yi * PEERS + ci, 8, along_y)
 
     lax.fori_loop(0, ORDER // KK, functools.partial(second_back, 1), 0)
     ones = jnp.ones((8, 128), F32)
@@ -444,15 +457,12 @@
         first_out[...] = first
         return
 
-    zi, xy = bi // 8, lax.rem(bi, 8)
-    along_z = lambda p: {"batch": p * 8 + xy}
-    in_plane = lambda p: {"batch": zi * 8 + p}
     issue(gath_z, 5, block, zi, 8, along_z)
-    first = collect(red_a, 7, PEERS)
-    issue(red_c, 8, first, xy, 8, in_plane)
+    first = collect(red_a, 7, 8)
+    issue(red_c, 8, first, xi, 4, along_x)
     landed(gath_z.at[pl.ds(0, 7)], recv_sem, 5)
     issue(gath, 6, gath_z[...], xy, 8, in_plane)
-    first = collect(red_c, 8, 8)
+    first = collect(red_c, 8, 4)
     issue(red_b, 9, first, zi, 8, along_z)
 
     whole = y_recv.at[pl.ds(0, (GROUPS - 1) * 16)]
@@ -476,8 +486,8 @@
         arrived(y_recv, send_sem, slot)
     landed(gath_z.at[pl.ds(0, 7)], send_sem, 5)
     landed(gath.at[pl.ds(0, 7)], send_sem, 6)
-    landed(red_a.at[pl.ds(0, PEERS - 1)], send_sem, 7)
-    landed(red_c.at[pl.ds(0, 7)], send_sem, 8)
+    landed(red_a.at[pl.ds(0, 7)], send_sem, 7)
+    landed(red_c.at[pl.ds(0, 3)], send_sem, 8)
     landed(red_b.at[pl.ds(0, 7)], send_sem, 9)
 
 
@@ -530,9 +540,9 @@
         pltpu.VMEM((ORDER, 128), F32),
         pltpu.VMEM((ORDER + 8, 128), F32),
         pltpu.VMEM((ORDER + 8, 128), F32),
-        pltpu.VMEM((PEERS, 17, 128), F32),
         pltpu.VMEM((8, 17, 128), F32),
         pltpu.VMEM((8, 17, 128), F32),
+        pltpu.VMEM((4, 17, 128), F32),
         pltpu.SemaphoreType.DMA((10,)),
         pltpu.SemaphoreType.DMA((10,)),
         pltpu.SemaphoreType.DMA((6 + len(NAMES),)),

time: 64.8 us -> 63.5 us (0.980)
  Pallas kernels: 64 us -> 62.7 us
    pallas_call x1, Pallas kernels: 63.2 us -> 61.9 us  [call(): pl.pallas_call(functools.partial(kernel, comm), out_shape=tuple((OUT(shap...]
where the time goes in v4:
time: 63.5 us; the launch traced here: 63.4 us
  Pallas kernels  62.7 us (99%)
  between operations  0.64 us (1%)
    pallas_call x1, Pallas kernels, call(): pl.pallas_call(functools.partial(kernel, comm), out_shape=tuple((OUT(shap...  61.9 us

profile of v4, /device:TPU:1, one launch (start us, length us, event | category | flops | bytes accessed | tf_op | source)
XLA Modules:
  0.0 63.4 jit_solution(1993279437958119546)
XLA Ops:
  0.6 61.9 %hyena_back.1 = (f32[256,512]{1,0:T(8,128)S(1)}, f32[33,64]{1,0:T(8,128)S(1)}, f32[64,256]{1,0:T(8,128)S(1)}, f32[1,256]{1,0:T(1,128)S(1)}, f32[1,256]{1,0:T(1,128)S(1)}) custom-call(f32[256,512]{1,0:T(8,128)} %refs_0_.1, f32[256,512]{1,0:T(8,128)} %refs_1_.1, f32[33,64]{1,0:T(8,128)} %refs_2_.1, f32[64,256]{1,0:T(8,128)} %refs_3_.1, f32[256]{0:T(256)} %refs_4_.1, ...), custom_call_target="tpu_custom_call" | custom-call | tf_op jit(solution)/shard_map/hyena_back/pallas_call | solution.py:555
  62.5 0.9 %finish.1 = (f32[256,512]{1,0:T(8,128)}, f32[33,64]{1,0:T(8,128)}, f32[64,256]{1,0:T(8,128)}, f32[1,256]{1,0:T(1,128)}, f32[1,256]{1,0:T(1,128)}) custom-call(f32[256,512]{1,0:T(8,128)S(1)} %get-tuple-element.15.refs_0_, f32[33,64]{1,0:T(8,128)S(1)} %get-tuple-element.16.refs_1_, f32[64,256]{1,0:T(8,128)S(1)} %get-tuple-element.17.refs_2_, ...), custom_call_target="tpu_custom_call" | custom-call | tf_op jit(solution)/shard_map/finish/pallas_call | solution.py:575

commit v5 on v4

--- a/solution.py
+++ b/solution.py
@@ -142,12 +142,15 @@
     ci = lax.axis_index("chan") if comm else 0
 
     def others(visit):
-        def step(i, _):
-            visit(lax.rem(bi + i, GROUPS))
+        def step(p, _):
+            visit(p)
             return 0
 
-        lax.fori_loop(GROUPS // 2, GROUPS, step, 0)
-        lax.fori_loop(1, GROUPS // 2, step, 0)
+        half = GROUPS // 2
+        lax.fori_loop(bi + half, GROUPS, step, 0)
+        lax.fori_loop(jnp.maximum(bi - half, 0), bi, step, 0)
+        lax.fori_loop(bi + 1, jnp.minimum(bi + half, GROUPS), step, 0)
+        lax.fori_loop(0, bi - half, step, 0)
 
     loads = [(cot_in, cot), (sig_in, sig), (first_in, weights), (second_in, cols), (rate_in, rate), (gain_in, gain)]
     loads += [(t_in[name], t[name]) for name in NAMES]

time: 63.5 us -> 63.3 us (level)
  no operation moved by 1% of the time
where the time goes in v5:
time: 63.3 us; the launch traced here: 63.2 us
  Pallas kernels  62.5 us (99%)
  between operations  0.64 us (1%)
    pallas_call x1, Pallas kernels, call(): pl.pallas_call(functools.partial(kernel, comm), out_shape=tuple((OUT(shap...  61.7 us

profile of v5, /device:TPU:1, one launch (start us, length us, event | category | flops | bytes accessed | tf_op | source)
XLA Modules:
  0.0 63.2 jit_solution(9484088117840324580)
XLA Ops:
  0.6 61.7 %hyena_back.1 = (f32[256,512]{1,0:T(8,128)S(1)}, f32[33,64]{1,0:T(8,128)S(1)}, f32[64,256]{1,0:T(8,128)S(1)}, f32[1,256]{1,0:T(1,128)S(1)}, f32[1,256]{1,0:T(1,128)S(1)}) custom-call(f32[256,512]{1,0:T(8,128)} %refs_0_.1, f32[256,512]{1,0:T(8,128)} %refs_1_.1, f32[33,64]{1,0:T(8,128)} %refs_2_.1, f32[64,256]{1,0:T(8,128)} %refs_3_.1, f32[256]{0:T(256)} %refs_4_.1, ...), custom_call_target="tpu_custom_call" | custom-call | tf_op jit(solution)/shard_map/hyena_back/pallas_call | solution.py:558
  62.3 0.9 %finish.1 = (f32[256,512]{1,0:T(8,128)}, f32[33,64]{1,0:T(8,128)}, f32[64,256]{1,0:T(8,128)}, f32[1,256]{1,0:T(1,128)}, f32[1,256]{1,0:T(1,128)}) custom-call(f32[256,512]{1,0:T(8,128)S(1)} %get-tuple-element.15.refs_0_, f32[33,64]{1,0:T(8,128)S(1)} %get-tuple-element.16.refs_1_, f32[64,256]{1,0:T(8,128)S(1)} %get-tuple-element.17.refs_2_, ...), custom_call_target="tpu_custom_call" | custom-call | tf_op jit(solution)/shard_map/finish/pallas_call | solution.py:578
